TPU v7x, 32 devices: a whole 2x2x4 slice. The times are simulated.
32 devices in a mesh: dp: 4 (over y, core), tensor: 8 (over z, x).
Axes of the slice: x: 2, y: 2, z: 4, core: 2. Of those that a mesh axis runs over, the one named last changes fastest.
Arguments:
- ref_hidden: bfloat16 [1152, 4608], P('dp', 'tensor'), may hold values from -6 to 6
- pol_hidden: bfloat16 [1152, 4608], P('dp', 'tensor'), may hold values from -6 to 6
- readout: bfloat16 [1152, 4608], P('dp', 'tensor'), may hold values from -0.019897461 to 0.019897461
- lengths: int32 [12], P('dp'), may hold values from 16 to 96, as said below
- pairing: int32 [12], replicated, may hold values from 0 to 11, each once
- pre_gain: float32 [4608], replicated, may hold values from 0.25 to 1.75
- post_gain: float32 [4608], replicated, may hold values from 0.25 to 1.75
- w_query: bfloat16 [4608, 4096], P('dp', 'tensor'), may hold values from -0.09375 to 0.09375
- w_key: bfloat16 [4608, 2048], P('dp', 'tensor'), may hold values from -3 to 3
- value_projection: bfloat16 [4608, 2048], P('dp', 'tensor'), may hold values from -0.09375 to 0.09375
- w_out: bfloat16 [4608, 4096], P('dp', 'tensor'), may hold values from -0.09375 to 0.09375
- a_query: bfloat16 [4608, 64], P('dp'), may hold values from -0.09375 to 0.09375
- a_value: bfloat16 [4608, 64], P('dp'), may hold values from -0.09375 to 0.09375
- query_second_factor: bfloat16 [64, 4096], P(None, 'tensor'), may hold values from -0.75 to 0.75
- value_second_factor: bfloat16 [64, 2048], P(None, 'tensor'), may hold values from -0.75 to 0.75
Outputs:
- policy_out: bfloat16 [1152, 4608], P('dp', 'tensor')
- reference_out: bfloat16 [1152, 4608], P('dp', 'tensor')
- dpo_loss: float32 [], replicated
- grad_hidden: bfloat16 [1152, 4608], P('dp', 'tensor')
- grad_a: float32 [4608, 128], P('dp')
- query_factor_gradient: float32 [64, 4096], P(None, 'tensor')
- value_factor_gradient: float32 [64, 2048], P(None, 'tensor')
Inputs may be any that keep to these rules, and one draw needn't show every extreme that they name: `lengths`: every sequence has at least one valid token and some sequence is full. `pairing`: entries 2k and 2k + 1 name the chosen and the rejected sequence of pair k; every sequence appears once.
All inputs are finite; a program needn't handle non-finite values.
Results may differ from a plain program's by a relative error of at most 0.0233.
The roundings to bfloat16 on the way count: a program that leaves them out, or rounds other values in their place, can miss the bound.
Values may be sent and summed in bfloat16 or wider, within the bound.
A program may use at most 128 MiB of HBM per device.

v0:
```python
import jax
import jax.numpy as jnp
from jax import lax
from jax.sharding import PartitionSpec as P

MODEL_WIDTH = 4608
HQ = 32
HEAD_SIZE = 128


NORM_EPS = 1e-06
SOFT_CAP = 50.0
ADAPTER_SCALE = 0.5
DPO_BETA = 0.5
LOSS_SCALE = 256.0
ROPE_BASE = 10000.0


def query_scale():
    return float(MODEL_WIDTH // HQ) ** (-0.5)


def apply_rotation(value_rows, direction):
    length = value_rows.shape[1]
    head_depth = value_rows.shape[3]
    middle = head_depth // 2
    spacing = ROPE_BASE ** (-2.0 * jnp.arange(middle, dtype=jnp.float32) / head_depth)
    angles = jnp.arange(length, dtype=jnp.float32)[:, None] * spacing[None, :]
    cosine = jnp.cos(angles)[None, :, None, :]
    sine_part = direction * jnp.sin(angles)[None, :, None, :]
    leading = value_rows[..., :middle]
    trailing = value_rows[..., middle:]
    return jnp.concatenate(
        [leading * cosine - trailing * sine_part, trailing * cosine + leading * sine_part], axis=-1
    )


def allowed_mask(lengths, length):
    places = jnp.arange(length)
    causal = places[None, :] <= places[:, None]
    living = places[None, :] < lengths[:, None]
    return causal[None, None, None, :, :] & living[:, None, None, None, :]


def attend(query_rows, rotated_keys, value_rows, lengths):
    seqs_here, length, q_heads, head_depth = query_rows.shape
    kv_heads = rotated_keys.shape[2]
    grouped_heads = query_rows.reshape(seqs_here, length, kv_heads, q_heads // kv_heads, head_depth)
    scores = (
        jnp.einsum(
            "sqkgd,spkd->skgqp", grouped_heads, rotated_keys, preferred_element_type=jnp.float32
        )
        * query_scale()
    )
    capped = SOFT_CAP * jnp.tanh(scores / SOFT_CAP)
    allowed = allowed_mask(lengths, length)
    weights = jnp.where(allowed, jnp.exp(capped), 0.0)
    probabilities = weights / jnp.sum(weights, axis=-1, keepdims=True)
    probs_low = probabilities.astype(jnp.bfloat16)
    mixed_out = jnp.einsum(
        "skgqp,spkd->sqkgd", probs_low, value_rows, preferred_element_type=jnp.float32
    )
    return (
        mixed_out.astype(jnp.bfloat16).reshape(seqs_here, length, q_heads, head_depth),
        probs_low,
        probabilities,
        capped,
    )


def attend_back(grad_mixed, query_rows, rotated_keys, value_rows, probs_low, probabilities, capped):
    seqs_here, length, q_heads, head_depth = query_rows.shape
    kv_heads = rotated_keys.shape[2]
    shape_five = (seqs_here, length, kv_heads, q_heads // kv_heads, head_depth)
    grouped_heads = query_rows.reshape(shape_five)
    grad_grouped = grad_mixed.reshape(shape_five)
    grad_probs = jnp.einsum(
        "sqkgd,spkd->skgqp", grad_grouped, value_rows, preferred_element_type=jnp.float32
    )
    value_rows_gradient = jnp.einsum(
        "skgqp,sqkgd->spkd", probs_low, grad_grouped, preferred_element_type=jnp.float32
    )
    centered = grad_probs - jnp.sum(grad_probs * probabilities, axis=-1, keepdims=True)
    grad_scores = (
        probabilities * centered * (1.0 - (capped / SOFT_CAP) ** 2) * query_scale()
    ).astype(jnp.bfloat16)
    query_rows_gradient = jnp.einsum(
        "skgqp,spkd->sqkgd", grad_scores, rotated_keys, preferred_element_type=jnp.float32
    ).reshape(seqs_here, length, q_heads, head_depth)
    key_rows_gradient = jnp.einsum(
        "skgqp,sqkgd->spkd", grad_scores, grouped_heads, preferred_element_type=jnp.float32
    )
    return (query_rows_gradient, key_rows_gradient, value_rows_gradient)


def normalize(hidden, pre_gain):
    whole_rows = lax.all_gather(hidden, "tensor", axis=1, tiled=True)
    wide_rows = whole_rows.astype(jnp.float32)
    pre_scale = lax.rsqrt(
        jnp.sum(wide_rows * wide_rows, axis=1, keepdims=True) / pre_gain.shape[0] + NORM_EPS
    )
    normed = (wide_rows * pre_scale * pre_gain).astype(jnp.bfloat16)
    return (normed, pre_scale)


def attention_layer(hidden, normed, weights, adapters, lengths, post_local):
    w_query, w_key, value_projection, w_out, a_query, a_value = weights
    tok_rows, full_width = normed.shape
    seqs_here = lengths.shape[0]
    length = tok_rows // seqs_here
    query_rows = jnp.dot(normed, w_query, preferred_element_type=jnp.float32)
    keys_before_rotation = jnp.dot(normed, w_key, preferred_element_type=jnp.float32)
    value_rows = jnp.dot(normed, value_projection, preferred_element_type=jnp.float32)
    low_rank_update = None
    if adapters is not None:
        query_second_factor, value_second_factor = adapters
        rank_size = query_second_factor.shape[0]
        low_rank_update = jnp.dot(
            normed, jnp.concatenate([a_query, a_value], axis=1), preferred_element_type=jnp.float32
        ).astype(jnp.bfloat16)
        query_rows = query_rows + ADAPTER_SCALE * jnp.dot(
            low_rank_update[:, :rank_size], query_second_factor, preferred_element_type=jnp.float32
        )
        value_rows = value_rows + ADAPTER_SCALE * jnp.dot(
            low_rank_update[:, rank_size:], value_second_factor, preferred_element_type=jnp.float32
        )
    q_heads = query_rows.shape[1] // HEAD_SIZE
    kv_heads = keys_before_rotation.shape[1] // HEAD_SIZE
    query_rows = apply_rotation(
        query_rows.reshape(seqs_here, length, q_heads, HEAD_SIZE), 1.0
    ).astype(jnp.bfloat16)
    rotated_keys = apply_rotation(
        keys_before_rotation.reshape(seqs_here, length, kv_heads, HEAD_SIZE), 1.0
    ).astype(jnp.bfloat16)
    value_rows = value_rows.reshape(seqs_here, length, kv_heads, HEAD_SIZE).astype(jnp.bfloat16)
    mixed_out, probs_low, probabilities, capped = attend(
        query_rows, rotated_keys, value_rows, lengths
    )
    head_terms = lax.dot_general(
        mixed_out.reshape(tok_rows, q_heads * HEAD_SIZE),
        w_out,
        (((1,), (1,)), ((), ())),
        preferred_element_type=jnp.float32,
    )
    summed = lax.psum_scatter(
        head_terms.astype(jnp.bfloat16), "tensor", scatter_dimension=1, tiled=True
    ).astype(jnp.float32)
    squares = lax.psum(jnp.sum(summed * summed, axis=1), "tensor")
    post_scale = lax.rsqrt(squares[:, None] / full_width + NORM_EPS)
    result = hidden.astype(jnp.float32) + summed * post_scale * post_local
    saved = (
        low_rank_update,
        query_rows,
        rotated_keys,
        value_rows,
        probs_low,
        probabilities,
        capped,
        summed,
        post_scale,
    )
    return (result, saved)


def body(
    ref_hidden,
    pol_hidden,
    readout,
    lengths,
    pairing,
    pre_gain,
    post_gain,
    w_query,
    w_key,
    value_projection,
    w_out,
    a_query,
    a_value,
    query_second_factor,
    value_second_factor,
):
    tok_rows, part_width = pol_hidden.shape
    seqs_here = lengths.shape[0]
    length = tok_rows // seqs_here
    tensor_rank = lax.axis_index("tensor")
    data_rank = lax.axis_index("dp")
    all_seqs = seqs_here * lax.axis_size("dp")
    full_width = part_width * lax.axis_size("tensor")
    pre_local = lax.dynamic_slice_in_dim(pre_gain, tensor_rank * part_width, part_width)
    post_local = lax.dynamic_slice_in_dim(post_gain, tensor_rank * part_width, part_width)
    weights = (
        lax.all_gather(w_query, "dp", axis=0, tiled=True),
        lax.all_gather(w_key, "dp", axis=0, tiled=True),
        lax.all_gather(value_projection, "dp", axis=0, tiled=True),
        lax.all_gather(w_out, "dp", axis=0, tiled=True),
        lax.all_gather(a_query, "dp", axis=0, tiled=True),
        lax.all_gather(a_value, "dp", axis=0, tiled=True),
    )
    w_query_all, w_key_all, w_value_all, w_out_all, a_query_all, a_value_all = weights
    ref_normed, ref_scale = normalize(ref_hidden, pre_gain)
    ref_result, ref_saved = attention_layer(
        ref_hidden, ref_normed, weights, None, lengths, post_local
    )
    pol_normed, pol_scale = normalize(pol_hidden, pre_gain)
    pol_result, pol_saved = attention_layer(
        pol_hidden,
        pol_normed,
        weights,
        (query_second_factor, value_second_factor),
        lengths,
        post_local,
    )
    readout_wide = readout.astype(jnp.float32)
    living = (jnp.arange(length)[None, :] < lengths[:, None]).astype(jnp.float32)

    def sequence_score(result):
        return jnp.sum(
            jnp.sum(result * readout_wide, axis=1).reshape(seqs_here, length) * living, axis=1
        )

    placed = jnp.zeros((2, all_seqs), jnp.float32)
    offset = data_rank * seqs_here
    placed = lax.dynamic_update_slice(
        placed,
        jnp.stack([sequence_score(ref_result), sequence_score(pol_result)]),
        (jnp.int32(0), offset),
    )
    scores = lax.psum(placed, ("dp", "tensor"))
    ratios = scores[1] - scores[0]
    chooser = (pairing[:, None] == jnp.arange(all_seqs)[None, :]).astype(jnp.float32)
    picked = jnp.dot(chooser, ratios, precision=lax.Precision.HIGHEST).reshape(-1, 2)
    margins = DPO_BETA * (picked[:, 0] - picked[:, 1])
    dpo_loss = jnp.sum(jax.nn.softplus(-margins))
    pair_pull = DPO_BETA * LOSS_SCALE * jax.nn.sigmoid(-margins)
    signed = jnp.stack([-pair_pull, pair_pull], axis=1).reshape(-1)
    coefficients = jnp.dot(signed, chooser, precision=lax.Precision.HIGHEST)
    local_coef = lax.dynamic_slice_in_dim(coefficients, offset, seqs_here)
    grad_result = (local_coef[:, None] * living).reshape(tok_rows, 1) * readout_wide
    (
        low_rank_update,
        query_rows,
        rotated_keys,
        value_rows,
        probs_low,
        probabilities,
        capped,
        summed,
        post_scale,
    ) = pol_saved
    post_dot = lax.psum(jnp.sum(summed * post_local * grad_result, axis=1), "tensor")
    grad_summed = (
        post_scale * post_local * grad_result
        - summed * post_scale**3 * post_dot[:, None] / full_width
    )
    grad_wide = lax.all_gather(grad_summed.astype(jnp.bfloat16), "tensor", axis=1, tiled=True)
    grad_mixed = jnp.dot(grad_wide, w_out_all, preferred_element_type=jnp.float32).astype(
        jnp.bfloat16
    )
    q_heads = query_rows.shape[2]
    grad_q_rot, rotated_key_gradient, value_head_gradient = attend_back(
        grad_mixed.reshape(seqs_here, length, q_heads, HEAD_SIZE),
        query_rows,
        rotated_keys,
        value_rows,
        probs_low,
        probabilities,
        capped,
    )
    query_rows_gradient = (
        apply_rotation(grad_q_rot, -1.0).reshape(tok_rows, -1).astype(jnp.bfloat16)
    )
    key_rows_gradient = (
        apply_rotation(rotated_key_gradient, -1.0).reshape(tok_rows, -1).astype(jnp.bfloat16)
    )
    value_rows_gradient = value_head_gradient.reshape(tok_rows, -1).astype(jnp.bfloat16)
    rank_size = query_second_factor.shape[0]
    rows_contraction = (((0,), (0,)), ((), ()))
    contract_cols = (((1,), (1,)), ((), ()))
    query_adapter_term = ADAPTER_SCALE * lax.dot_general(
        low_rank_update[:, :rank_size],
        query_rows_gradient,
        rows_contraction,
        preferred_element_type=jnp.float32,
    )
    value_adapter_term = ADAPTER_SCALE * lax.dot_general(
        low_rank_update[:, rank_size:],
        value_rows_gradient,
        rows_contraction,
        preferred_element_type=jnp.float32,
    )
    query_factor_gradient, value_factor_gradient = (
        lax.psum(query_adapter_term.astype(jnp.bfloat16), "dp").astype(jnp.float32),
        lax.psum(value_adapter_term.astype(jnp.bfloat16), "dp").astype(jnp.float32),
    )
    adapter_grad = jnp.concatenate(
        [
            ADAPTER_SCALE
            * lax.dot_general(
                query_rows_gradient,
                query_second_factor,
                contract_cols,
                preferred_element_type=jnp.float32,
            ),
            ADAPTER_SCALE
            * lax.dot_general(
                value_rows_gradient,
                value_second_factor,
                contract_cols,
                preferred_element_type=jnp.float32,
            ),
        ],
        axis=1,
    ).astype(jnp.bfloat16)
    adapter_term = lax.dot_general(
        pol_normed, adapter_grad, rows_contraction, preferred_element_type=jnp.float32
    )
    adapter_part = lax.psum_scatter(
        adapter_term.astype(jnp.bfloat16), "dp", scatter_dimension=0, tiled=True
    )
    grad_a = lax.psum(adapter_part, "tensor").astype(jnp.float32)
    a_both = jnp.concatenate([a_query_all, a_value_all], axis=1)
    input_terms = lax.dot_general(
        query_rows_gradient, w_query_all, contract_cols, preferred_element_type=jnp.float32
    )
    input_terms = input_terms + lax.dot_general(
        key_rows_gradient, w_key_all, contract_cols, preferred_element_type=jnp.float32
    )
    input_terms = input_terms + lax.dot_general(
        value_rows_gradient, w_value_all, contract_cols, preferred_element_type=jnp.float32
    )
    input_terms = input_terms + lax.dot_general(
        adapter_grad, a_both, contract_cols, preferred_element_type=jnp.float32
    )
    input_whole = lax.psum(input_terms.astype(jnp.bfloat16), "tensor").astype(jnp.float32)
    grad_normed = lax.dynamic_slice_in_dim(input_whole, tensor_rank * part_width, part_width, 1)
    narrow = pol_hidden.astype(jnp.float32)
    pre_dot = lax.psum(jnp.sum(narrow * pre_local * grad_normed, axis=1), "tensor")
    grad_hidden = (
        grad_result
        + pol_scale * pre_local * grad_normed
        - narrow * pol_scale**3 * pre_dot[:, None] / full_width
    )
    return (
        pol_result.astype(jnp.bfloat16),
        ref_result.astype(jnp.bfloat16),
        dpo_loss,
        grad_hidden.astype(jnp.bfloat16),
        grad_a,
        query_factor_gradient,
        value_factor_gradient,
    )


def solution(mesh):
    placed = (
        P("dp", "tensor"),
        P("dp", "tensor"),
        P("dp", "tensor"),
        P("dp"),
        P(),
        P(),
        P(),
        P("dp", "tensor"),
        P("dp", "tensor"),
        P("dp", "tensor"),
        P("dp", "tensor"),
        P("dp", None),
        P("dp", None),
        P(None, "tensor"),
        P(None, "tensor"),
    )
    return jax.shard_map(
        body,
        mesh=mesh,
        in_specs=placed,
        out_specs=(
            P("dp", "tensor"),
            P("dp", "tensor"),
            P(),
            P("dp", "tensor"),
            P("dp", None),
            P(None, "tensor"),
            P(None, "tensor"),
        ),
        check_vma=False,
    )
```

profile of v0, /device:TPU:0, one launch (start us, length us, event | category | flops | bytes accessed | tf_op | source)
XLA Modules:
  0.0 823.7 jit_solution(8016594998505936199)
XLA Ops:
  11.2 9.0 %all_gather.29 = bf16[4608,64]{0,1:T(8,128)(2,1)S(1)} all-gather(bf16[1152,64]{0,1:T(8,128)(2,1)S(1)} %copy-done.29), channel_id=1, replica_groups=mesh['dp'=4,'tensor'=8] {'dp'}, dimensions={0}, use_global_device_ids=true | all-gather | bytes 737280 | tf_op jit(solution)/shard_map/all_gather | solution.py:196
  20.3 7.6 all_gather.30
  29.8 41.2 %all-gather.21.cloned.1.call-done = bf16[8,576,288]{1,2,0:T(8,128)(2,1)} async-done(((bf16[1,576,288]{1,2,0:T(8,128)(2,1)}), bf16[8,576,288]{1,2,0:T(8,128)(2,1)}) %all-gather.21.cloned.1.call-update) | async-done | bytes 2654224 | tf_op jit(solution)/shard_map/all_gather | solution.py:97
  71.0 5.3 copy.72
  76.4 7.2 reshape.270
  83.6 46.3 %all-gather.19.cloned.1.call-done = bf16[8,576,288]{1,2,0:T(8,128)(2,1)} async-done(((bf16[1,576,288]{1,2,0:T(8,128)(2,1)}), bf16[8,576,288]{1,2,0:T(8,128)(2,1)}) %all-gather.19.cloned.1.call-update) | async-done | bytes 2654224 | tf_op jit(solution)/shard_map/all_gather | solution.py:97
  129.8 5.3 copy.64
  135.2 7.5 reshape.269
  142.7 3.1 multiply_reduce_fusion
  147.8 1.5 copy-done.1
  149.3 3.3 multiply_convert_fusion
  152.6 1.5 all-gather.13.cloned.1.call-done
  154.1 3.3 fusion.141
  157.6 3.2 fusion.139
  160.8 1.1 reshape.255
  162.0 17.7 %all-gather.11.cloned.1.call-done = bf16[4608,256]{1,0:T(8,128)(2,1)} async-done(((bf16[1152,256]{1,0:T(8,128)(2,1)}), bf16[4608,256]{1,0:T(8,128)(2,1)}) %all-gather.11.cloned.1.call-update) | async-done | bytes 2359312 | tf_op jit(solution)/shard_map/all_gather | solution.py:194
  179.6 3.3 convolution_convert_fusion.6
  186.1 32.4 %all-gather.15.cloned.1.call-done = bf16[4608,512]{1,0:T(8,128)(2,1)} async-done(((bf16[1152,512]{1,0:T(8,128)(2,1)}), bf16[4608,512]{1,0:T(8,128)(2,1)}) %all-gather.15.cloned.1.call-update) | async-done | bytes 4718608 | tf_op jit(solution)/shard_map/all_gather | solution.py:192
  218.5 5.5 fusion.142
  224.0 1.3 reshape.258
  225.2 4.4 fusion.140
  230.6 2.1 reshape.256
  232.7 2.9 subtract_convert_fusion.1
  235.8 1.3 fusion.12
  237.1 1.5 fusion.15
  239.0 18.4 %all-gather.17.cloned.1.call-done = bf16[4608,512]{1,0:T(8,128)(2,1)} async-done(((bf16[1152,512]{1,0:T(8,128)(2,1)}), bf16[4608,512]{1,0:T(8,128)(2,1)}) %all-gather.17.cloned.1.call-update) | async-done | bytes 4718608 | tf_op jit(solution)/shard_map/all_gather | solution.py:195
  257.4 5.4 convolution_convert_fusion
  262.8 4.7 copy.110
  267.9 2.5 fusion.138
  272.4 1.6 fusion.54
  276.2 5.6 convolution_convert_fusion.1
  281.8 4.7 copy.108
  288.0 59.1 %reduce-scatter.12.cloned.1.call-done = bf16[576,288]{1,0:T(8,128)(2,1)} async-done(((bf16[4608,288]{1,0:T(8,128)(2,1)}), bf16[576,288]{1,0:T(8,128)(2,1)}) %reduce-scatter.12.cloned.1.call-update) | async-done | bytes 331792
  347.1 1.9 copy.111
  349.1 80.7 %reduce-scatter.10.cloned.1.call-done = bf16[576,288]{1,0:T(8,128)(2,1)} async-done(((bf16[4608,288]{1,0:T(8,128)(2,1)}), bf16[576,288]{1,0:T(8,128)(2,1)}) %reduce-scatter.10.cloned.1.call-update) | async-done | bytes 331792
  429.8 1.2 copy.109
  431.2 1.2 fusion.32
  432.3 20.1 %all-reduce = (f32[288]{0:T(512)S(1)}, f32[288]{0:T(512)S(1)}) all-reduce(f32[288]{0:T(512)S(1)} %fusion.45, f32[288]{0:T(512)S(1)} %fusion.32), channel_id=1, replica_groups=mesh['dp'=4,'tensor'=8] {'tensor'}, use_global_device_ids=true, to_apply=%region_4.5 | all-reduce | flops 576 | bytes 4608 | tf_op jit(solution)/shard_map/psum | solution.py:148
  452.4 2.6 fusion.43
  456.9 36.8 %psum.65 = f32[2,12]{1,0:T(2,128)S(1)} all-reduce(f32[2,12]{1,0:T(2,128)S(1)} %dynamic_update_slice.3), channel_id=1, replica_groups=mesh['dp'=4,'tensor'=8] {'dp','tensor'}, use_global_device_ids=true, to_apply=%region_14.15 | all-reduce | flops 24 | bytes 192 | tf_op jit(solution)/shard_map/psum | solution.py:228
  496.7 21.1 %psum.66 = f32[288]{0:T(512)S(1)} all-reduce(f32[288]{0:T(512)S(1)} %fusion.38), channel_id=1, replica_groups=mesh['dp'=4,'tensor'=8] {'tensor'}, use_global_device_ids=true, to_apply=%region_17.18 | all-reduce | flops 288 | bytes 2304 | tf_op jit(solution)/shard_map/psum | solution.py:250
  517.9 1.1 fusion.55
  519.2 55.1 %all-gather.23.cloned.1.call-done = bf16[8,576,288]{1,2,0:T(8,128)(2,1)} async-done(((bf16[1,576,288]{1,2,0:T(8,128)(2,1)}), bf16[8,576,288]{1,2,0:T(8,128)(2,1)}) %all-gather.23.cloned.1.call-update) | async-done | bytes 2654224 | tf_op jit(solution)/shard_map/all_gather | solution.py:255
  574.3 4.4 copy.82
  578.7 5.6 reshape.268
  584.4 5.4 convolution_convert_fusion.3
  589.8 1.0 reshape_reshape.11
  590.8 2.1 convolution_bitcast_fusion
  592.9 2.0 fusion.19
  594.9 3.3 fusion.27
  598.2 1.5 fusion.135
  602.8 2.2 convolution_convert_fusion.2
  605.1 2.5 convolution_bitcast_fusion.2
  609.0 4.3 fusion.58
  616.2 2.4 fusion.1
  618.7 10.8 %reduce-scatter.8.cloned.1.call-done = bf16[1152,128]{1,0:T(8,128)(2,1)} async-done(((bf16[4608,128]{1,0:T(8,128)(2,1)}), bf16[1152,128]{1,0:T(8,128)(2,1)}) %reduce-scatter.8.cloned.1.call-update) | async-done | bytes 294928 | tf_op jit(solution)/shard_map/reduce_scatter | solution.py:317
  631.2 10.5 %psum.71 = bf16[64,256]{1,0:T(8,128)(2,1)S(1)} all-reduce(bf16[64,256]{1,0:T(8,128)(2,1)S(1)} %fusion.23), channel_id=1, replica_groups=mesh['dp'=4,'tensor'=8] {'dp'}, use_global_device_ids=true, to_apply=%region_25.26 | all-reduce | flops 16384 | bytes 65536 | tf_op jit(solution)/shard_map/psum | solution.py:293
  642.3 21.6 %all-reduce.5.cloned.1.call-done = bf16[64,512]{1,0:T(8,128)(2,1)} async-done(((bf16[64,512]{1,0:T(8,128)(2,1)}), bf16[64,512]{1,0:T(8,128)(2,1)}) %all-reduce.5.cloned.1.call-update) | async-done | bytes 65552 | tf_op jit(solution)/shard_map/psum | solution.py:292
  664.0 1.5 convert_element_type.173
  665.5 126.0 %all-reduce.7.cloned.1.call-done = (bf16[288,4608]{1,0:T(8,128)(2,1)}, bf16[1152,128]{1,0:T(8,128)(2,1)}) async-done(((bf16[288,4608]{1,0:T(8,128)(2,1)}, bf16[1152,128]{1,0:T(8,128)(2,1)}), (bf16[288,4608]{1,0:T(8,128)(2,1)}, bf16[1152,128]{1,0:T(8,128)(2,1)})) %all-reduce.7.cloned.1.call-update) | async-done | bytes 2949136 | tf_op jit(solution)/shard_map/psum | solution.py:334
  791.4 1.3 fusion.35
  792.8 19.4 %psum.68 = f32[288]{0:T(512)S(1)} all-reduce(f32[288]{0:T(512)S(1)} %fusion.35), channel_id=1, replica_groups=mesh['dp'=4,'tensor'=8] {'tensor'}, use_global_device_ids=true, to_apply=%region_21.22 | all-reduce | flops 288 | bytes 2304 | tf_op jit(solution)/shard_map/psum | solution.py:337
  812.2 1.8 convert_element_type.171
  814.0 2.4 fusion.40
  (179 shorter events, 33.5 us)
Async XLA Ops:
  7.2 222.4 %copy-start = (bf16[64,512]{1,0:T(8,128)(2,1)S(1)}, bf16[64,512]{1,0:T(8,128)(2,1)}, u32[]{:S(2)}) copy-start(bf16[64,512]{1,0:T(8,128)(2,1)} %param.28) | copy-start | bytes 196612
  7.2 4.1 copy-start.29
  7.2 63.8 %all-gather.21.cloned.1.call-start = ((), (), s32[]{:S(2)}) async-start(), calls=%async_computation.10 | async-start | bytes 3317760 | tf_op jit(solution)/shard_map/all_gather | solution.py:97
  7.9 121.9 %all-gather.19.cloned.1.call-start = ((), (), s32[]{:S(2)}) async-start(), calls=%async_computation.9 | async-start | bytes 3317760 | tf_op jit(solution)/shard_map/all_gather | solution.py:97
  8.7 11.6 %copy-start.30 = (bf16[1152,64]{0,1:T(8,128)(2,1)S(1)}, bf16[1152,64]{0,1:T(8,128)(2,1)}, u32[]{:S(2)}) copy-start(bf16[1152,64]{0,1:T(8,128)(2,1)} %param.27) | copy-start | bytes 442372
  8.7 145.4 %all-gather.13.cloned.1.call-start = ((), (), s32[]{:S(2)}) async-start(), calls=%async_computation.4 | async-start | bytes 2949120 | tf_op jit(solution)/shard_map/all_gather | solution.py:193
  9.4 170.2 %all-gather.11.cloned.1.call-start = ((), (), s32[]{:S(2)}) async-start(), calls=%async_computation.3 | async-start | bytes 2949120 | tf_op jit(solution)/shard_map/all_gather | solution.py:194
  10.0 18.0 %copy-start.40 = (s32[3]{0:T(128)S(1)}, s32[3]{0:T(128)}, u32[]{:S(2)}) copy-start(s32[3]{0:T(128)} %param.18) | copy-start | bytes 40
  10.0 208.5 %all-gather.15.cloned.1.call-start = ((), (), s32[]{:S(2)}) async-start(), calls=%async_computation.5 | async-start | bytes 5898240 | tf_op jit(solution)/shard_map/all_gather | solution.py:192
  10.6 246.8 %all-gather.17.cloned.1.call-start = ((), (), s32[]{:S(2)}) async-start(), calls=%async_computation.6 | async-start | bytes 5898240 | tf_op jit(solution)/shard_map/all_gather | solution.py:195
  11.2 336.0 %reduce-scatter.12.cloned.1.call-start = ((), (), s32[]{:S(2)}) async-start(), calls=%async_computation.13 | async-start | bytes 3981312
  28.1 48.3 %copy-start.3 = (bf16[4608,128]{0,1:T(8,128)(2,1)}, bf16[4608,128]{0,1:T(8,128)(2,1)S(1)}, u32[]{:S(2)}) copy-start(bf16[4608,128]{0,1:T(8,128)(2,1)S(1)} %constant_dynamic-update-slice_fusion) | copy-start | bytes 3538948
  29.8 202.9 %copy-start.12 = (f32[96,64]{1,0:T(8,128)}, f32[96,64]{1,0:T(8,128)S(1)}, u32[]{:S(2)}) copy-start(f32[96,64]{1,0:T(8,128)S(1)} %get-tuple-element.50) | copy-start | bytes 73732
  135.2 12.6 %copy-start.36 = (f32[4608]{0:T(1024)S(1)}, f32[4608]{0:T(1024)}, u32[]{:S(2)}) copy-start(f32[4608]{0:T(1024)} %param.20) | copy-start | bytes 55300
  142.7 4.1 copy-start.2
  146.8 2.5 copy-start.1
  147.8 4.9 copy-start.37
  183.6 1.6 copy-start.4
  232.7 3.0 copy-start.25
  232.7 3.0 copy-start.26
  232.7 3.0 copy-start.31
  235.7 1.4 copy-start.27
  267.6 2.8 copy-start.34
  267.6 4.7 copy-start.15
  267.6 4.7 copy-start.14
  267.6 162.2 %reduce-scatter.10.cloned.1.call-start = ((), (), s32[]{:S(2)}) async-start(), calls=%async_computation.12 | async-start | bytes 3981312
  272.2 2.9 copy-start.16
  272.3 2.6 copy-start.32
  272.3 1.7 copy-start.19
  272.4 3.9 copy-start.20
  274.0 0.8 copy-start.43
  274.0 0.8 copy-start.44
  286.5 0.7 copy-start.41
  286.5 165.9 %copy-start.6 = (bf16[288,576]{1,0:T(8,128)(2,1)S(1)}, bf16[288,576]{1,0:T(8,128)(2,1)}, u32[]{:S(2)}) copy-start(bf16[288,576]{1,0:T(8,128)(2,1)} %param.17) | copy-start | bytes 995332
  286.5 287.8 %all-gather.23.cloned.1.call-start = ((), (), s32[]{:S(2)}) async-start(), calls=%async_computation.11 | async-start | bytes 3317760 | tf_op jit(solution)/shard_map/all_gather | solution.py:255
  518.9 110.6 %reduce-scatter.8.cloned.1.call-start = ((), (), s32[]{:S(2)}) async-start(), calls=%async_computation.7 | async-start | bytes 1474560 | tf_op jit(solution)/shard_map/reduce_scatter | solution.py:317
  584.4 8.5 %copy-start.33 = (pred[3,96,96]{1,2,0:T(8,128)(4,1)S(1)}, pred[3,96,96]{1,2,0:T(8,128)(4,1)}, u32[]{:S(2)}) copy-start(pred[3,96,96]{1,2,0:T(8,128)(4,1)} %broadcast_and_fusion) | copy-start | bytes 82948
  584.4 8.5 %copy-start.45 = (f32[3,2,2,96]{3,2,1,0:T(2,128)S(1)}, f32[3,2,2,96]{3,2,1,0:T(2,128)}, u32[]{:S(2)}) copy-start(f32[3,2,2,96]{3,2,1,0:T(2,128)} %copy-done.44) | copy-start | bytes 13828
  594.9 4.8 copy-start.28
  594.9 5.6 copy-start.35
  594.9 5.8 copy-start.13
  594.9 5.8 copy-start.17
  599.8 0.7 copy-start.10
  600.7 1.5 copy-start.21
  602.2 0.6 copy-start.23
  605.0 2.6 copy-start.18
  605.1 58.9 %all-reduce.5.cloned.1.call-start = ((), (), s32[]{:S(2)}) async-start(), calls=%async_computation.8 | async-start | bytes 131072 | tf_op jit(solution)/shard_map/psum | solution.py:292
  608.9 4.3 copy-start.8
  608.9 182.5 %all-reduce.7.cloned.1.call-start = ((), (), s32[]{:S(2)}) async-start(), calls=%async_computation.14 | async-start | bytes 5898240 | tf_op jit(solution)/shard_map/psum | solution.py:334
  613.3 1.7 copy-start.9
  613.3 1.7 copy-start.11
  614.9 1.3 copy-start.5
  614.9 1.3 copy-start.22
  614.9 1.3 copy-start.24
  618.7 11.6 %copy-start.42 = (f32[6,1]{0,1:T(1,128)S(1)}, f32[6,1]{0,1:T(1,128)}, u32[]{:S(2)}) copy-start(f32[6,1]{0,1:T(1,128)} %get-tuple-element.17) | copy-start | bytes 76
  618.7 172.8 %copy-start.7 = (bf16[288,576]{1,0:T(8,128)(2,1)S(1)}, bf16[288,576]{1,0:T(8,128)(2,1)}, u32[]{:S(2)}) copy-start(bf16[288,576]{1,0:T(8,128)(2,1)} %param.16) | copy-start | bytes 995332
  618.7 195.4 %copy-start.38 = (f32[288]{0:T(512)S(1)}, f32[288]{0:T(512)}, u32[]{:S(2)}) copy-start(f32[288]{0:T(512)} %copy-done.37) | copy-start | bytes 3460
  618.7 195.4 %copy-start.39 = (f32[288]{0:T(512)S(1)}, f32[288]{0:T(512)}, u32[]{:S(2)}) copy-start(f32[288]{0:T(512)} %get-tuple-element.44) | copy-start | bytes 3460
Sparse Core Ops, SparseCore 0:
  10.2 60.8 all-gather.20
  73.2 56.5 all-gather.18
  131.4 22.6 all-gather.12
  155.5 24.0 all-gather.10
  181.0 37.4 all-gather.14
  219.9 37.4 all-gather.16
  267.7 79.4 reduce-scatter.11
  350.8 78.9 reduce-scatter.9
  519.1 55.2 all-gather.22
  605.2 24.2 reduce-scatter.7
  632.4 31.5 all-reduce.4
  667.5 123.9 all-reduce.6
where the time goes:
time: 829 us; the launch traced here: 824 us
  waiting for transfers between devices  515 us (62%)
  blocking collectives  125 us (15%)
  matrix products  69.4 us (8%)
  local copies, waits for them, and re-layouts  68.6 us (8%)
  other arithmetic  30.4 us (4%)
  between operations  15.3 us (2%)
    unnamed x14, waiting for transfers between devices  144 us
    psum x1, waiting for transfers between devices, body(): lax.psum(input_terms.astype(jnp.bfloat16), 'tensor').astype(jnp.float32)  126 us
    all_gather x2, waiting for transfers between devices, normalize(): whole_rows = lax.all_gather(hidden, 'tensor', axis=1, tiled=True)  87.5 us
    all_gather x1, waiting for transfers between devices, body(): lax.all_gather(grad_summed.astype(jnp.bfloat16), 'tensor', axis=1, tiled=...  55.1 us
    psum x1, blocking collectives, body(): scores = lax.psum(placed, ('dp', 'tensor'))  36.8 us
    all_gather x1, waiting for transfers between devices, body(): lax.all_gather(w_query, 'dp', axis=0, tiled=True)  32.4 us
    convert_element_type x4, local copies, waits for them, and re-layouts, normalize(): wide_rows = whole_rows.astype(jnp.float32)  25.3 us
    unnamed x98, local copies, waits for them, and re-layouts  24.6 us
  transfers between devices with their start and end apart: 12, of which 12 were waited for; matrix products, arithmetic and copies ran while one was open for 13% of the time, Pallas kernels for 0%

commit v1 on v0

v1 whole, which is shorter than its diff:
```python
import jax
import jax.numpy as jnp
from jax import lax
from jax.experimental import pallas as pl
from jax.experimental.pallas import tpu as pltpu
from jax.sharding import PartitionSpec as P

MODEL_WIDTH = 4608
HQ = 32
HEAD_SIZE = 128


NORM_EPS = 1e-06
SOFT_CAP = 50.0
ADAPTER_SCALE = 0.5
DPO_BETA = 0.5
LOSS_SCALE = 256.0
ROPE_BASE = 10000.0


def query_scale():
    return float(MODEL_WIDTH // HQ) ** (-0.5)


def apply_rotation(value_rows, direction):
    length = value_rows.shape[1]
    head_depth = value_rows.shape[3]
    middle = head_depth // 2
    spacing = ROPE_BASE ** (-2.0 * jnp.arange(middle, dtype=jnp.float32) / head_depth)
    angles = jnp.arange(length, dtype=jnp.float32)[:, None] * spacing[None, :]
    cosine = jnp.cos(angles)[None, :, None, :]
    sine_part = direction * jnp.sin(angles)[None, :, None, :]
    leading = value_rows[..., :middle]
    trailing = value_rows[..., middle:]
    return jnp.concatenate(
        [leading * cosine - trailing * sine_part, trailing * cosine + leading * sine_part], axis=-1
    )


def allowed_mask(lengths, length):
    places = jnp.arange(length)
    causal = places[None, :] <= places[:, None]
    living = places[None, :] < lengths[:, None]
    return causal[None, None, None, :, :] & living[:, None, None, None, :]


def attend(query_rows, rotated_keys, value_rows, lengths):
    seqs_here, length, q_heads, head_depth = query_rows.shape
    kv_heads = rotated_keys.shape[2]
    grouped_heads = query_rows.reshape(seqs_here, length, kv_heads, q_heads // kv_heads, head_depth)
    scores = (
        jnp.einsum(
            "sqkgd,spkd->skgqp", grouped_heads, rotated_keys, preferred_element_type=jnp.float32
        )
        * query_scale()
    )
    capped = SOFT_CAP * jnp.tanh(scores / SOFT_CAP)
    allowed = allowed_mask(lengths, length)
    weights = jnp.where(allowed, jnp.exp(capped), 0.0)
    probabilities = weights / jnp.sum(weights, axis=-1, keepdims=True)
    probs_low = probabilities.astype(jnp.bfloat16)
    mixed_out = jnp.einsum(
        "skgqp,spkd->sqkgd", probs_low, value_rows, preferred_element_type=jnp.float32
    )
    return (
        mixed_out.astype(jnp.bfloat16).reshape(seqs_here, length, q_heads, head_depth),
        probs_low,
        probabilities,
        capped,
    )


def attend_back(grad_mixed, query_rows, rotated_keys, value_rows, probs_low, probabilities, capped):
    seqs_here, length, q_heads, head_depth = query_rows.shape
    kv_heads = rotated_keys.shape[2]
    shape_five = (seqs_here, length, kv_heads, q_heads // kv_heads, head_depth)
    grouped_heads = query_rows.reshape(shape_five)
    grad_grouped = grad_mixed.reshape(shape_five)
    grad_probs = jnp.einsum(
        "sqkgd,spkd->skgqp", grad_grouped, value_rows, preferred_element_type=jnp.float32
    )
    value_rows_gradient = jnp.einsum(
        "skgqp,sqkgd->spkd", probs_low, grad_grouped, preferred_element_type=jnp.float32
    )
    centered = grad_probs - jnp.sum(grad_probs * probabilities, axis=-1, keepdims=True)
    grad_scores = (
        probabilities * centered * (1.0 - (capped / SOFT_CAP) ** 2) * query_scale()
    ).astype(jnp.bfloat16)
    query_rows_gradient = jnp.einsum(
        "skgqp,spkd->sqkgd", grad_scores, rotated_keys, preferred_element_type=jnp.float32
    ).reshape(seqs_here, length, q_heads, head_depth)
    key_rows_gradient = jnp.einsum(
        "skgqp,sqkgd->spkd", grad_scores, grouped_heads, preferred_element_type=jnp.float32
    )
    return (query_rows_gradient, key_rows_gradient, value_rows_gradient)


MESH = pl.DeviceIdType.MESH
VMEM_GRANT = 60 * 2**20


def grid_of(axis, count):
    if axis == "dp":
        inner = 2 if count % 2 == 0 else 1
    else:
        inner = 1
        while (inner * 2) ** 2 <= count and count % (inner * 2) == 0:
            inner *= 2
    return count // inner, inner


def row_chunk(rows):
    for size in (48, 32, 16):
        if rows % size == 0:
            return size
    return rows


class Place:
    def __init__(self, axis, count):
        self.axis = axis
        self.outer, self.inner = grid_of(axis, count)
        rank = lax.axis_index(axis)
        self.a = lax.div(rank, self.inner)
        self.b = lax.rem(rank, self.inner)
        self.rank = rank

    def out_at(self, j):
        return lax.rem(self.a + j + self.outer, self.outer)

    def in_at(self, k):
        return lax.rem(self.b + k + self.inner, self.inner)

    def slot(self, j, k):
        return self.out_at(j) * self.inner + self.in_at(k)

    def peers(self):
        return [self.slot(j, 0) for j in range(1, self.outer)] + [
            self.slot(0, k) for k in range(1, self.inner)
        ]


def remote(src, dst, send_sem, recv_sem, axis, rank):
    return pltpu.make_async_remote_copy(
        src_ref=src,
        dst_ref=dst,
        send_sem=send_sem,
        recv_sem=recv_sem,
        device_id={axis: rank},
        device_id_type=MESH,
    )


def communicate(name, number, counts, gathers=(), reduces=(), gain=None):
    places_used = sorted({axis for _, axis, _ in gathers} | ({"tensor"} if reduces else set()))
    tensor_count = counts["tensor"]
    operands, in_specs, out_shapes, out_specs, scratch = [], [], [], [], []
    vmem = pl.BlockSpec(memory_space=pltpu.VMEM)
    plan = []
    for array, axis, kind in gathers:
        operands.append(array)
        in_specs.append(vmem)
        whole = (counts[axis],) + array.shape
        outer, inner = grid_of(axis, counts[axis])
        entry = {"axis": axis, "kind": kind, "x": len(operands) - 1}
        if kind in ("vmem", "hbm"):
            entry["out"] = len(out_shapes)
            out_shapes.append(jax.ShapeDtypeStruct(whole, array.dtype))
            out_specs.append(vmem if kind == "vmem" else pl.BlockSpec(memory_space=pl.ANY))
        else:
            entry["held"] = len(scratch)
            scratch.append(pltpu.VMEM(whole, array.dtype))
            entry["out"] = len(out_shapes)
            out_shapes.append(
                jax.ShapeDtypeStruct((array.shape[0], array.shape[1] * counts[axis]), jnp.bfloat16)
            )
            out_specs.append(vmem)
            if kind == "norm":
                out_shapes.append(jax.ShapeDtypeStruct((array.shape[0], 1), jnp.float32))
                out_specs.append(vmem)
                entry["gain"] = len(operands)
                operands.append(gain.reshape(1, -1))
                in_specs.append(vmem)
        entry["sems"] = len(scratch)
        n_outer, n_inner = max(outer - 1, 1), max(outer * (inner - 1), 1)
        scratch += [
            pltpu.SemaphoreType.DMA((n_outer,)),
            pltpu.SemaphoreType.DMA((n_outer,)),
            pltpu.SemaphoreType.DMA((n_inner,)),
            pltpu.SemaphoreType.DMA((n_inner,)),
            pltpu.SemaphoreType.DMA,
        ]
        plan.append(entry)
    sums = []
    for array in reduces:
        rows, width = array.shape
        outer, inner = grid_of("tensor", tensor_count)
        part = width // tensor_count
        n_inner = max(outer * (inner - 1), 1)
        sums.append({"x": len(operands), "out": len(out_shapes), "scratch": len(scratch)})
        operands.append(array)
        in_specs.append(vmem)
        out_shapes.append(jax.ShapeDtypeStruct((rows, part), jnp.float32))
        out_specs.append(vmem)
        scratch += [
            pltpu.VMEM((tensor_count, rows, part), array.dtype),
            pltpu.VMEM((n_inner, rows, part), array.dtype),
            pltpu.VMEM((outer, rows, part), array.dtype),
            pltpu.VMEM((outer, rows, part), array.dtype),
            pltpu.SemaphoreType.DMA((n_inner,)),
            pltpu.SemaphoreType.DMA((n_inner,)),
            pltpu.SemaphoreType.DMA((outer,)),
            pltpu.SemaphoreType.DMA((outer,)),
        ]
    n_in, n_out = len(operands), len(out_shapes)

    def kernel(*refs):
        ins, outs, work = refs[:n_in], refs[n_in : n_in + n_out], refs[n_in + n_out :]
        places = {axis: Place(axis, counts[axis]) for axis in places_used}
        barrier = pltpu.get_barrier_semaphore()
        total = 0
        for axis, place in places.items():
            for peer in place.peers():
                pl.semaphore_signal(barrier, inc=1, device_id={axis: peer}, device_id_type=MESH)
                total += 1
        pl.semaphore_wait(barrier, total)
        for entry in plan:
            place = places[entry["axis"]]
            x = ins[entry["x"]]
            held = work[entry["held"]] if "held" in entry else outs[entry["out"]]
            so, ro, si, ri, own_sem = work[entry["sems"] : entry["sems"] + 5]
            entry["far"], entry["near"] = [], []
            mine = held.at[place.rank]
            for j in range(1, place.outer):
                copy = remote(
                    x, mine, so.at[j - 1], ro.at[j - 1], place.axis, place.slot(j, 0)
                )
                copy.start()
                entry["far"].append(copy)
            for k in range(1, place.inner):
                copy = remote(
                    x, mine, si.at[k - 1], ri.at[k - 1], place.axis, place.slot(0, k)
                )
                copy.start()
                entry["near"].append(copy)
            entry["own"] = pltpu.make_async_copy(x, mine, own_sem)
            entry["own"].start()
        for item in sums:
            place = places["tensor"]
            x = ins[item["x"]]
            stage, near_box, outgoing, far_box, si, ri, so, ro = work[
                item["scratch"] : item["scratch"] + 8
            ]
            part = stage.shape[2]
            rows = stage.shape[1]
            size = row_chunk(rows)

            @pl.loop(0, rows // size)
            def _(step, x=x, stage=stage, part=part, size=size):
                at = pl.ds(pl.multiple_of(step * size, size), size)
                for n in range(tensor_count):
                    stage[n, at, :] = x[at, n * part : (n + 1) * part]

            item["near"], item["far"] = {}, {}
            for j in [*range(1, place.outer), 0]:
                for k in range(1, place.inner):
                    at = j * (place.inner - 1) + k - 1
                    copy = remote(
                        stage.at[place.slot(j, k)],
                        near_box.at[at],
                        si.at[at],
                        ri.at[at],
                        "tensor",
                        place.slot(0, k),
                    )
                    copy.start()
                    item["near"][j, k] = copy
        for item in sums:
            place = places["tensor"]
            out = outs[item["out"]]
            stage, near_box, outgoing, far_box, si, ri, so, ro = work[
                item["scratch"] : item["scratch"] + 8
            ]
            rows = stage.shape[1]
            size = row_chunk(rows)
            for j in [*range(1, place.outer), 0]:
                for k in range(1, place.inner):
                    item["near"][j, k].wait_recv()

                @pl.loop(0, rows // size)
                def _(step, j=j):
                    at = pl.ds(pl.multiple_of(step * size, size), size)
                    value = stage[place.slot(j, 0), at, :].astype(jnp.float32)
                    for k in range(1, place.inner):
                        value += near_box[j * (place.inner - 1) + k - 1, at, :].astype(jnp.float32)
                    if j:
                        outgoing[j, at, :] = value.astype(outgoing.dtype)
                    else:
                        out[at, :] = value

                if j:
                    copy = remote(
                        outgoing.at[j], far_box.at[j], so.at[j], ro.at[j], "tensor", place.slot(j, 0)
                    )
                    copy.start()
                    item["far"][j] = copy
        for entry in plan:
            place = places[entry["axis"]]
            held = work[entry["held"]] if "held" in entry else outs[entry["out"]]
            so, ro, si, ri, own_sem = work[entry["sems"] : entry["sems"] + 5]
            for j in range(1, place.outer):
                entry["far"][j - 1].wait_recv()
                block = held.at[place.slot(-j, 0)]
                for k in range(1, place.inner):
                    at = j * (place.inner - 1) + k - 1
                    copy = remote(
                        block, block, si.at[at], ri.at[at], place.axis, place.slot(0, k)
                    )
                    copy.start()
                    entry["near"].append(copy)
            if "held" in entry:
                finish(entry, ins, outs, held)
        for item in sums:
            out = outs[item["out"]]
            far_box = work[item["scratch"] + 3]
            rows = out.shape[0]
            size = row_chunk(rows)
            for copy in item["far"].values():
                copy.wait_recv()

            @pl.loop(0, rows // size)
            def _(step, out=out, far_box=far_box, size=size, item=item):
                at = pl.ds(pl.multiple_of(step * size, size), size)
                value = out[at, :]
                for j in item["far"]:
                    value += far_box[j, at, :].astype(jnp.float32)
                out[at, :] = value

            for copy in [*item["near"].values(), *item["far"].values()]:
                copy.wait_send()
        for entry in plan:
            if "held" not in entry:
                for copy in entry["near"]:
                    copy.wait_recv()
                entry["own"].wait()
            for copy in entry["near"] + entry["far"]:
                copy.wait_send()

    def finish(entry, ins, outs, held):
        for copy in entry["near"]:
            copy.wait_recv()
        entry["own"].wait()
        count, rows, part = held.shape
        out = outs[entry["out"]]
        size = row_chunk(rows)

        @pl.loop(0, rows // size)
        def _(step):
            at = pl.ds(pl.multiple_of(step * size, size), size)
            if entry["kind"] == "rows":
                for n in range(count):
                    out[at, n * part : (n + 1) * part] = held[n, at, :].astype(out.dtype)
                return
            square = jnp.zeros((size, part), jnp.float32)
            for n in range(count):
                value = held[n, at, :].astype(jnp.float32)
                square += value * value
            scale = lax.rsqrt(
                jnp.sum(square, axis=1, keepdims=True) / (count * part) + NORM_EPS
            )
            outs[entry["out"] + 1][at, :] = scale
            gain_ref = ins[entry["gain"]]
            for n in range(count):
                cols = slice(n * part, (n + 1) * part)
                value = held[n, at, :].astype(jnp.float32)
                out[at, cols] = (value * scale * gain_ref[:, cols]).astype(out.dtype)

    return pl.pallas_call(
        kernel,
        name=name,
        out_shape=out_shapes,
        in_specs=in_specs,
        out_specs=out_specs,
        scratch_shapes=scratch,
        compiler_params=pltpu.CompilerParams(
            collective_id=number, has_side_effects=True, vmem_limit_bytes=VMEM_GRANT
        ),
    )(*operands)


def body(
    ref_hidden,
    pol_hidden,
    readout,
    lengths,
    pairing,
    pre_gain,
    post_gain,
    w_query,
    w_key,
    value_projection,
    w_out,
    a_query,
    a_value,
    query_second_factor,
    value_second_factor,
):
    f32, bf16 = jnp.float32, jnp.bfloat16
    tok_rows, part_width = pol_hidden.shape
    seqs_here = lengths.shape[0]
    length = tok_rows // seqs_here
    tensor_rank = lax.axis_index("tensor")
    data_rank = lax.axis_index("dp")
    counts = {"dp": lax.axis_size("dp"), "tensor": lax.axis_size("tensor")}
    all_seqs = seqs_here * counts["dp"]
    full_width = part_width * counts["tensor"]
    rank_size = query_second_factor.shape[0]
    rows_contraction = (((0,), (0,)), ((), ()))
    contract_cols = (((1,), (1,)), ((), ()))

    def dot(a, b, dims=(((1,), (0,)), ((), ()))):
        return lax.dot_general(a, b, dims, preferred_element_type=f32)

    pre_local = lax.dynamic_slice_in_dim(pre_gain, tensor_rank * part_width, part_width)
    post_local = lax.dynamic_slice_in_dim(post_gain, tensor_rank * part_width, part_width)
    hidden = jnp.concatenate([ref_hidden, pol_hidden], axis=0)
    gathered = communicate(
        "gather_inputs",
        1,
        counts,
        gathers=[
            (jnp.concatenate([a_query, a_value], axis=1), "dp", "hbm"),
            (w_query, "dp", "hbm"),
            (hidden, "tensor", "norm"),
            (w_key, "dp", "hbm"),
            (value_projection, "dp", "hbm"),
            (w_out, "dp", "hbm"),
        ],
        gain=pre_gain,
    )
    a_both, w_query_all, normed, pre_scale, w_key_all, w_value_all, w_out_all = [
        v.reshape(-1, v.shape[-1]) for v in gathered
    ]
    pol_normed = normed[tok_rows:]
    pol_scale = pre_scale[tok_rows:]
    low_rank_update = dot(pol_normed, a_both).astype(bf16)
    query_rows = dot(normed, w_query_all)
    keys_before_rotation = dot(normed, w_key_all)
    value_rows = dot(normed, w_value_all)
    added_query = ADAPTER_SCALE * dot(low_rank_update[:, :rank_size], query_second_factor)
    added_value = ADAPTER_SCALE * dot(low_rank_update[:, rank_size:], value_second_factor)
    none = ((tok_rows, 0), (0, 0))
    query_rows = query_rows + jnp.pad(added_query, none)
    value_rows = value_rows + jnp.pad(added_value, none)
    q_heads = query_rows.shape[1] // HEAD_SIZE
    kv_heads = value_rows.shape[1] // HEAD_SIZE
    both = 2 * seqs_here
    query_rows = apply_rotation(
        query_rows.reshape(both, length, q_heads, HEAD_SIZE), 1.0
    ).astype(bf16)
    rotated_keys = apply_rotation(
        keys_before_rotation.reshape(both, length, kv_heads, HEAD_SIZE), 1.0
    ).astype(bf16)
    value_rows = value_rows.reshape(both, length, kv_heads, HEAD_SIZE).astype(bf16)
    mixed_out, probs_low, probabilities, capped = attend(
        query_rows, rotated_keys, value_rows, jnp.concatenate([lengths, lengths])
    )
    head_terms = dot(
        mixed_out.reshape(2 * tok_rows, q_heads * HEAD_SIZE), w_out_all, contract_cols
    ).astype(bf16)
    (summed_both,) = communicate("scatter_out", 2, counts, reduces=[head_terms])
    readout_wide = readout.astype(f32)
    living = (jnp.arange(length)[None, :] < lengths[:, None]).astype(f32)
    weighted = post_local * readout_wide
    shaped = summed_both.reshape(2, tok_rows, part_width)
    hidden_wide = hidden.astype(f32).reshape(2, tok_rows, part_width)
    stats = jnp.concatenate(
        [
            jnp.sum(shaped * shaped, axis=2),
            jnp.sum(shaped * weighted, axis=2),
            jnp.sum(hidden_wide * readout_wide, axis=2),
            jnp.zeros((2, tok_rows), f32),
        ],
        axis=0,
    )
    (stats_all,) = communicate("token_sums", 3, counts, gathers=[(stats, "tensor", "vmem")])
    stats = jnp.sum(stats_all, axis=0)
    post_scale = lax.rsqrt(stats[0:2] / full_width + NORM_EPS)
    token_scores = (stats[4:6] + post_scale * stats[2:4]).reshape(2, seqs_here, length) * living
    mine = jnp.sum(token_scores, axis=2)
    mine = jnp.pad(mine, ((0, 6), (0, 128 - seqs_here)))
    (scores_all,) = communicate("sequence_scores", 4, counts, gathers=[(mine, "dp", "vmem")])
    scores = jnp.transpose(scores_all[:, :2, :seqs_here], (1, 0, 2)).reshape(2, all_seqs)
    ratios = scores[1] - scores[0]
    chooser = (pairing[:, None] == jnp.arange(all_seqs)[None, :]).astype(f32)
    picked = jnp.sum(chooser * ratios[None, :], axis=1).reshape(-1, 2)
    margins = DPO_BETA * (picked[:, 0] - picked[:, 1])
    dpo_loss = jnp.sum(jax.nn.softplus(-margins))
    pair_pull = DPO_BETA * LOSS_SCALE * jax.nn.sigmoid(-margins)
    signed = jnp.stack([-pair_pull, pair_pull], axis=1).reshape(-1)
    coefficients = jnp.sum(signed[:, None] * chooser, axis=0)
    local_coef = lax.dynamic_slice_in_dim(coefficients, data_rank * seqs_here, seqs_here)
    token_coef = (local_coef[:, None] * living).reshape(tok_rows)
    grad_result = token_coef[:, None] * readout_wide
    post_dot = token_coef * stats[3]
    summed = shaped[1]
    scale_col = post_scale[1][:, None]
    result = hidden_wide + shaped * post_scale[:, :, None] * post_local
    grad_summed = (
        scale_col * post_local * grad_result
        - summed * scale_col**3 * post_dot[:, None] / full_width
    ).astype(bf16)
    (grad_wide,) = communicate("gather_grad", 5, counts, gathers=[(grad_summed, "tensor", "rows")])
    grad_mixed = dot(grad_wide, w_out_all).astype(bf16)
    grad_q_rot, rotated_key_gradient, value_head_gradient = attend_back(
        grad_mixed.reshape(seqs_here, length, q_heads, HEAD_SIZE),
        query_rows[seqs_here:],
        rotated_keys[seqs_here:],
        value_rows[seqs_here:],
        probs_low[seqs_here:],
        probabilities[seqs_here:],
        capped[seqs_here:],
    )
    query_rows_gradient = apply_rotation(grad_q_rot, -1.0).reshape(tok_rows, -1).astype(bf16)
    key_rows_gradient = (
        apply_rotation(rotated_key_gradient, -1.0).reshape(tok_rows, -1).astype(bf16)
    )
    value_rows_gradient = value_head_gradient.reshape(tok_rows, -1).astype(bf16)
    factor_terms = ADAPTER_SCALE * jnp.concatenate(
        [
            dot(low_rank_update[:, :rank_size], query_rows_gradient, rows_contraction),
            dot(low_rank_update[:, rank_size:], value_rows_gradient, rows_contraction),
        ],
        axis=1,
    )
    hook_terms = ADAPTER_SCALE * jnp.concatenate(
        [
            dot(query_rows_gradient, query_second_factor, contract_cols),
            dot(value_rows_gradient, value_second_factor, contract_cols),
        ],
        axis=1,
    )
    hook_all, factor_all = communicate(
        "adapter_sums",
        6,
        counts,
        gathers=[
            (hook_terms.astype(bf16), "tensor", "vmem"),
            (factor_terms.astype(bf16), "dp", "vmem"),
        ],
    )
    factor_gradient = jnp.sum(factor_all.astype(f32), axis=0)
    query_factor_gradient = factor_gradient[:, : query_second_factor.shape[1]]
    value_factor_gradient = factor_gradient[:, query_second_factor.shape[1] :]
    hook = jnp.sum(hook_all.astype(f32), axis=0).astype(bf16)
    adapter_term = dot(pol_normed, hook, rows_contraction)
    slice_rows = full_width // (counts["dp"] * counts["tensor"])
    adapter_term = adapter_term.reshape(counts["dp"], counts["tensor"], slice_rows, -1)
    adapter_mine = lax.dynamic_index_in_dim(adapter_term, tensor_rank, 1, keepdims=False)
    input_terms = (
        dot(query_rows_gradient, w_query_all, contract_cols)
        + dot(key_rows_gradient, w_key_all, contract_cols)
        + dot(value_rows_gradient, w_value_all, contract_cols)
    ).astype(bf16)
    adapter_blocks, grad_normed = communicate(
        "scatter_grad",
        7,
        counts,
        gathers=[(adapter_mine.astype(bf16), "dp", "vmem")],
        reduces=[input_terms],
    )
    adapter_rows = jnp.sum(
        lax.dynamic_index_in_dim(adapter_blocks, data_rank, 1, keepdims=False).astype(f32), axis=0
    )
    a_local = lax.dynamic_slice_in_dim(a_both, tensor_rank * part_width, part_width)
    grad_normed = grad_normed + dot(hook, a_local, contract_cols)
    narrow = pol_hidden.astype(f32)
    pre_sums = jnp.sum(narrow * pre_local * grad_normed, axis=1)
    pre_sums = jnp.pad(pre_sums[None, :], ((0, 7), (0, 0)))
    adapter_all, pre_all = communicate(
        "last_sums",
        8,
        counts,
        gathers=[(adapter_rows.astype(bf16), "tensor", "vmem"), (pre_sums, "tensor", "vmem")],
    )
    grad_a = adapter_all.reshape(-1, adapter_all.shape[-1]).astype(f32)
    pre_dot = jnp.sum(pre_all[:, 0, :], axis=0)
    grad_hidden = (
        grad_result
        + pol_scale * pre_local * grad_normed
        - narrow * pol_scale**3 * pre_dot[:, None] / full_width
    )
    return (
        result[1].astype(bf16),
        result[0].astype(bf16),
        dpo_loss,
        grad_hidden.astype(bf16),
        grad_a,
        query_factor_gradient,
        value_factor_gradient,
    )


def solution(mesh):
    placed = (
        P("dp", "tensor"),
        P("dp", "tensor"),
        P("dp", "tensor"),
        P("dp"),
        P(),
        P(),
        P(),
        P("dp", "tensor"),
        P("dp", "tensor"),
        P("dp", "tensor"),
        P("dp", "tensor"),
        P("dp", None),
        P("dp", None),
        P(None, "tensor"),
        P(None, "tensor"),
    )
    return jax.shard_map(
        body,
        mesh=mesh,
        in_specs=placed,
        out_specs=(
            P("dp", "tensor"),
            P("dp", "tensor"),
            P(),
            P("dp", "tensor"),
            P("dp", None),
            P(None, "tensor"),
            P(None, "tensor"),
        ),
        check_vma=False,
    )
```

time: 829 us -> 457 us (0.55)
  waiting for transfers between devices: 515 us -> 0 us
  Pallas kernels: 0 us -> 353 us
  blocking collectives: 125 us -> 0 us
  local copies, waits for them, and re-layouts: 68.6 us -> 28.7 us
  matrix products: 69.4 us -> 51.3 us
  between operations: 15.3 us -> 1.31 us
    pallas_call x0 -> x8, Pallas kernels: none -> 353 us  [communicate(): pl.pallas_call(kernel, name=name, out_shape=out_shapes, in_specs=in_specs...]
    all_gather x7 -> x0, waiting for transfers between devices: 213 us -> none  [the longest x2 87.5 us: normalize(): whole_rows = lax.all_gather(hidden, 'tensor', axis=1, tiled=True)]
    psum x2 -> x0, waiting for transfers between devices: 148 us -> none  [the longest x1 126 us: body(): lax.psum(input_terms.astype(jnp.bfloat16), 'tensor').astype(jnp.float32)]
    unnamed x14 -> x0, waiting for transfers between devices: 144 us -> none
    psum x5 -> x0, blocking collectives: 108 us -> none  [the longest x1 36.8 us: body(): scores = lax.psum(placed, ('dp', 'tensor'))]
    convert_element_type x7 -> x4, local copies, waits for them, and re-layouts: 27.1 us -> 1.79 us  [the longest x1 0.92 us: body(): result[0].astype(bf16)]
    unnamed x98 -> x57, local copies, waits for them, and re-layouts: 24.6 us -> 4.77 us
    all_gather x2 -> x0, blocking collectives: 16.7 us -> none  [the longest x1 9.03 us: body(): lax.all_gather(a_query, 'dp', axis=0, tiled=True)]
  transfers between devices with their start and end apart: 12 -> 0, of which waited for: 12 -> 0; matrix products, arithmetic and copies ran while one was open for 13% -> 0% of each run, Pallas kernels for 0% -> 0%
where the time goes in v1:
time: 457 us; the launch traced here: 456 us
  Pallas kernels  353 us (77%)
  matrix products  51.3 us (11%)
  local copies, waits for them, and re-layouts  28.7 us (6%)
  other arithmetic  22.3 us (5%)
    pallas_call x8, Pallas kernels, communicate(): pl.pallas_call(kernel, name=name, out_shape=out_shapes, in_specs=in_specs...  353 us
    dot_general x17, matrix products, dot(): return lax.dot_general(a, b, dims, preferred_element_type=f32)  44.2 us

profile of v1, /device:TPU:0, one launch (start us, length us, event | category | flops | bytes accessed | tf_op | source)
XLA Modules:
  0.0 456.3 jit_solution(14686139267956111784)
XLA Ops:
  0.7 0.8 pad_add_fusion
  2.1 0.7 fusion.99
  2.9 0.8 dynamic_slice.20
  3.6 0.8 dynamic_slice.22
  4.4 1.3 reshape.314.refs_3_
  6.1 1.1 copy.83
  7.3 1.1 copy.84
  8.4 0.9 pad_maximum_fusion.1.refs_0_
  9.4 1.2 mul.555
  11.6 101.0 %gather_inputs.1 = (bf16[4,1152,128]{2,1,0:T(8,128)(2,1)}, bf16[4,1152,512]{2,1,0:T(8,128)(2,1)}, bf16[576,4608]{1,0:T(8,128)(2,1)}, f32[576,1]{1,0:T(8,128)}, b...) custom-call(bf16[1152,128]{1,0:T(8,128)(2,1)} %pad_maximum_fusion.1.refs_0_, ...), custom_call_target="tpu_custom_call" | custom-call | tf_op jit(solution)/shard_map/gather_inputs/pallas_call | solution.py:378
  112.6 1.1 slice_reduce_fusion
  113.7 3.1 fusion.20
  117.0 4.0 fusion.17
  121.4 6.3 %convolution_add_fusion.2 = f32[576,512]{1,0:T(8,128)S(1)} fusion(bf16[576,4608]{1,0:T(8,128)(2,1)} %get-tuple-element.20, bf16[4608,512]{1,0:T(8,128)(2,1)} %bitcast.129, f32[288,512]{1,0:T(8,128)S(1)} %convolution_multiply_fusion.1), kind=kOutput, calls=%fused_computation.20 | convolution fusion | flops 2718203904 | bytes 11796480 | tf_op jit(solution)/shard_map/dot_general | solution.py:422
  128.1 0.8 subtract_convert_fusion
  129.4 0.9 copy.86
  130.3 0.9 copy.87
  131.2 0.8 copy.102
  132.0 2.5 copy.85
  134.5 4.3 fusion.116
  139.1 0.7 copy-done.15
  140.1 0.9 fusion.24
  141.0 1.4 fusion.113
  143.2 1.0 reshape_reshape.6
  144.3 1.9 slice_bitcast_fusion
  146.2 3.0 copy.91
  149.2 7.8 %convolution_convert_fusion.refs_0_ = bf16[576,4608]{1,0:T(8,128)(2,1)} fusion(bf16[576,512]{1,0:T(8,128)(2,1)} %reshape_reshape.6, bf16[4608,512]{1,0:T(8,128)(2,1)} %bitcast.148), kind=kOutput, calls=%fused_computation.1 | convolution fusion | flops 2720563200 | bytes 10616832 | tf_op jit(solution)/shard_map/dot_general | solution.py:422
  157.0 104.8 %scatter_out.1 = f32[576,576]{1,0:T(8,128)} custom-call(bf16[576,4608]{1,0:T(8,128)(2,1)} %convolution_convert_fusion.refs_0_), custom_call_target="tpu_custom_call" | custom-call | tf_op jit(solution)/shard_map/scatter_out/pallas_call | solution.py:378
  261.8 2.3 multiply_reduce_fusion.1
  264.3 0.7 maximum_maximum_fusion.refs_0_
  264.9 10.4 %token_sums.1 = f32[8,8,288]{2,1,0:T(8,128)} custom-call(f32[8,288]{1,0:T(8,128)} %maximum_maximum_fusion.refs_0_), custom_call_target="tpu_custom_call" | custom-call | tf_op jit(solution)/shard_map/token_sums/pallas_call | solution.py:378
  275.4 0.9 reduce_sum.151
  276.7 0.9 slice_bitcast_fusion.1
  278.4 5.8 %sequence_scores.1 = f32[4,8,128]{2,1,0:T(8,128)} custom-call(f32[8,128]{1,0:T(8,128)} %pad.18.refs_0_), custom_call_target="tpu_custom_call" | custom-call | tf_op jit(solution)/shard_map/sequence_scores/pallas_call | solution.py:378
  284.2 0.7 slice_bitcast_fusion.3
  285.5 0.6 fusion.101
  286.6 1.0 subtract_convert_fusion.1.refs_0_
  287.6 47.9 %gather_grad.1 = bf16[288,4608]{1,0:T(8,128)(2,1)} custom-call(bf16[288,576]{1,0:T(8,128)(2,1)} %subtract_convert_fusion.1.refs_0_), custom_call_target="tpu_custom_call" | custom-call | tf_op jit(solution)/shard_map/gather_grad/pallas_call | solution.py:378
  335.6 5.4 %convolution_convert_fusion.2 = bf16[288,512]{1,0:T(8,128)(2,1)} fusion(bf16[288,4608]{1,0:T(8,128)(2,1)} %gather_grad.1, bf16[4608,512]{1,0:T(8,128)(2,1)} %bitcast.149), kind=kOutput, calls=%fused_computation.31 | convolution fusion | flops 1359101952 | bytes 7667712 | tf_op jit(solution)/shard_map/dot_general | solution.py:422
  341.0 1.1 reshape_reshape.7
  342.9 1.2 convolution_bitcast_fusion
  344.0 2.2 fusion.25
  346.3 2.2 convolution_bitcast_fusion.1
  349.3 0.8 multiply_subtract_fusion
  350.7 0.7 fusion.68.refs_1_
  351.6 0.7 fusion.81.refs_0_
  352.3 4.1 fusion.47
  356.4 0.9 convolution_add_fusion.1
  357.3 0.8 copy-done.10
  358.1 2.4 fusion.1.refs_1_
  360.5 22.4 %adapter_sums.1 = (bf16[8,288,128]{2,1,0:T(8,128)(2,1)}, bf16[4,64,768]{2,1,0:T(8,128)(2,1)}) custom-call(bf16[288,128]{1,0:T(8,128)(2,1)} %fusion.81.refs_0_, bf16[64,768]{1,0:T(8,128)(2,1)} %fusion.68.refs_1_), custom_call_target="tpu_custom_call" | custom-call | tf_op jit(solution)/shard_map/adapter_sums/pallas_call | solution.py:378
  382.9 1.1 reduce_sum.157
  384.1 3.1 fusion.2
  387.1 0.7 fusion.73.refs_0_
  387.8 44.5 %scatter_grad.1 = (bf16[4,4,144,128]{3,2,1,0:T(8,128)(2,1)}, f32[288,576]{1,0:T(8,128)}) custom-call(bf16[4,144,128]{2,1,0:T(8,128)(2,1)} %fusion.73.refs_0_, bf16[288,4608]{1,0:T(8,128)(2,1)} %fusion.1.refs_1_), custom_call_target="tpu_custom_call" | custom-call | tf_op jit(solution)/shard_map/scatter_grad/pallas_call | solution.py:378
  432.3 1.6 fusion.35
  433.9 0.6 pad.19.refs_1_
  434.6 1.6 dynamic-slice_reduce_fusion.refs_0_
  436.2 0.6 slice.173
  436.8 0.7 slice.172
  437.5 15.9 %last_sums.1 = (bf16[8,144,128]{2,1,0:T(8,128)(2,1)}, f32[8,8,288]{2,1,0:T(8,128)}) custom-call(bf16[144,128]{1,0:T(8,128)(2,1)} %dynamic-slice_reduce_fusion.refs_0_, f32[8,288]{1,0:T(8,128)} %pad.19.refs_1_), custom_call_target="tpu_custom_call" | custom-call | tf_op jit(solution)/shard_map/last_sums/pallas_call | solution.py:378
  453.4 1.0 slice_reduce_fusion.1
  454.4 1.1 fusion.33
  455.4 0.9 bitcast_convert_fusion
  (109 shorter events, 9.6 us)
Async XLA Ops:
  0.6 120.6 %copy-start = (bf16[64,512]{1,0:T(8,128)(2,1)S(1)}, bf16[64,512]{1,0:T(8,128)(2,1)}, u32[]{:S(2)}) copy-start(bf16[64,512]{1,0:T(8,128)(2,1)} %param.28) | copy-start | bytes 196612
  0.6 8.6 %copy-start.6 = (bf16[288,576]{1,0:T(8,128)(2,1)S(1)}, bf16[288,576]{1,0:T(8,128)(2,1)}, u32[]{:S(2)}) copy-start(bf16[288,576]{1,0:T(8,128)(2,1)} %param.17) | copy-start | bytes 995332
  9.3 1.3 copy-start.18
  9.3 1.3 copy-start.8
  10.7 0.9 copy-start.4
  113.7 3.1 copy-start.22
  113.7 3.3 copy-start.9
  129.4 2.6 copy-start.2
  138.8 1.1 copy-start.15
  138.8 1.3 copy-start.16
  139.1 1.9 copy-start.19
  139.1 1.9 copy-start.20
  141.0 1.4 copy-start.13
  142.4 0.8 copy-start.11
  261.8 2.5 copy-start.25
  261.8 14.5 %copy-start.1 = (f32[576,576]{1,0:T(8,128)S(1)}, f32[576,576]{1,0:T(8,128)}, u32[]{:S(2)}) copy-start(f32[576,576]{1,0:T(8,128)} %scatter_out.1) | copy-start | bytes 3981316
  261.8 14.5 %copy-start.5 = (bf16[576,576]{1,0:T(8,128)(2,1)S(1)}, bf16[576,576]{1,0:T(8,128)(2,1)}, u32[]{:S(2)}) copy-start(bf16[576,576]{1,0:T(8,128)(2,1)} %copy-done.4) | copy-start | bytes 1990660
  276.6 8.4 %copy-start.26 = (s32[12]{0:T(128)S(1)}, s32[12]{0:T(128)}, u32[]{:S(2)}) copy-start(s32[12]{0:T(128)} %param.19) | copy-start | bytes 148
  276.6 9.8 %copy-start.24 = (s32[3]{0:T(128)S(1)}, s32[3]{0:T(128)}, u32[]{:S(2)}) copy-start(s32[3]{0:T(128)} %param.18) | copy-start | bytes 40
  276.7 9.9 %copy-start.7 = (bf16[288,576]{1,0:T(8,128)(2,1)S(1)}, bf16[288,576]{1,0:T(8,128)(2,1)}, u32[]{:S(2)}) copy-start(bf16[288,576]{1,0:T(8,128)(2,1)} %param.17) | copy-start | bytes 995332
  335.6 6.6 %copy-start.12 = (bf16[6,2,2,96,96]{3,4,2,1,0:T(8,128)(2,1)S(1)}, bf16[6,2,2,96,96]{3,4,2,1,0:T(8,128)(2,1)}, u32[]{:S(2)}) copy-start(bf16[6,2,2,96,96]{3,4,2,1,0:T(8,128)(2,1)} %copy-done.11) | copy-start | bytes 1327108
  341.0 3.0 copy-start.14
  346.3 2.6 copy-start.23
  352.3 4.1 copy-start.3
  356.4 1.7 copy-start.10
  432.3 3.8 copy-start.17
  453.4 2.0 copy-start.21

commit v2 on v1

--- a/solution.py
+++ b/solution.py
@@ -111,6 +111,13 @@
 
 def row_chunk(rows):
     for size in (48, 32, 16):
+        if rows % size == 0:
+            return size
+    return rows
+
+
+def piece_rows(rows):
+    for size in range(96, 0, -16):
         if rows % size == 0:
             return size
     return rows
@@ -182,7 +189,10 @@
                 operands.append(gain.reshape(1, -1))
                 in_specs.append(vmem)
         entry["sems"] = len(scratch)
-        n_outer, n_inner = max(outer - 1, 1), max(outer * (inner - 1), 1)
+        size = piece_rows(array.shape[0]) if "held" in entry else array.shape[0]
+        entry["size"], entry["pieces"] = size, array.shape[0] // size
+        n_outer = max(outer - 1, 1) * entry["pieces"]
+        n_inner = max(outer * (inner - 1), 1) * entry["pieces"]
         scratch += [
             pltpu.SemaphoreType.DMA((n_outer,)),
             pltpu.SemaphoreType.DMA((n_outer,)),
@@ -196,8 +206,18 @@
         rows, width = array.shape
         outer, inner = grid_of("tensor", tensor_count)
         part = width // tensor_count
+        size = piece_rows(rows)
+        pieces = rows // size
         n_inner = max(outer * (inner - 1), 1)
-        sums.append({"x": len(operands), "out": len(out_shapes), "scratch": len(scratch)})
+        sums.append(
+            {
+                "x": len(operands),
+                "out": len(out_shapes),
+                "scratch": len(scratch),
+                "size": size,
+                "pieces": pieces,
+            }
+        )
         operands.append(array)
         in_specs.append(vmem)
         out_shapes.append(jax.ShapeDtypeStruct((rows, part), jnp.float32))
@@ -207,10 +227,10 @@
             pltpu.VMEM((n_inner, rows, part), array.dtype),
             pltpu.VMEM((outer, rows, part), array.dtype),
             pltpu.VMEM((outer, rows, part), array.dtype),
-            pltpu.SemaphoreType.DMA((n_inner,)),
-            pltpu.SemaphoreType.DMA((n_inner,)),
-            pltpu.SemaphoreType.DMA((outer,)),
-            pltpu.SemaphoreType.DMA((outer,)),
+            pltpu.SemaphoreType.DMA((n_inner * pieces,)),
+            pltpu.SemaphoreType.DMA((n_inner * pieces,)),
+            pltpu.SemaphoreType.DMA((outer * pieces,)),
+            pltpu.SemaphoreType.DMA((outer * pieces,)),
         ]
     n_in, n_out = len(operands), len(out_shapes)
 
@@ -231,18 +251,32 @@
             so, ro, si, ri, own_sem = work[entry["sems"] : entry["sems"] + 5]
             entry["far"], entry["near"] = [], []
             mine = held.at[place.rank]
-            for j in range(1, place.outer):
-                copy = remote(
-                    x, mine, so.at[j - 1], ro.at[j - 1], place.axis, place.slot(j, 0)
-                )
-                copy.start()
-                entry["far"].append(copy)
-            for k in range(1, place.inner):
-                copy = remote(
-                    x, mine, si.at[k - 1], ri.at[k - 1], place.axis, place.slot(0, k)
-                )
-                copy.start()
-                entry["near"].append(copy)
+            for c in range(entry["pieces"]):
+                rows = pl.ds(c * entry["size"], entry["size"])
+                for j in range(1, place.outer):
+                    at = c * (place.outer - 1) + j - 1
+                    copy = remote(
+                        x.at[rows],
+                        mine.at[rows],
+                        so.at[at],
+                        ro.at[at],
+                        place.axis,
+                        place.slot(j, 0),
+                    )
+                    copy.start()
+                    entry["far"].append(copy)
+                for k in range(1, place.inner):
+                    at = c * place.outer * (place.inner - 1) + k - 1
+                    copy = remote(
+                        x.at[rows],
+                        mine.at[rows],
+                        si.at[at],
+                        ri.at[at],
+                        place.axis,
+                        place.slot(0, k),
+                    )
+                    copy.start()
+                    entry["near"].append(copy)
             entry["own"] = pltpu.make_async_copy(x, mine, own_sem)
             entry["own"].start()
         for item in sums:
@@ -252,89 +286,103 @@
                 item["scratch"] : item["scratch"] + 8
             ]
             part = stage.shape[2]
-            rows = stage.shape[1]
-            size = row_chunk(rows)
-
-            @pl.loop(0, rows // size)
-            def _(step, x=x, stage=stage, part=part, size=size):
-                at = pl.ds(pl.multiple_of(step * size, size), size)
-                for n in range(tensor_count):
-                    stage[n, at, :] = x[at, n * part : (n + 1) * part]
-
+            size = row_chunk(item["size"])
+            n_near = place.outer * (place.inner - 1)
             item["near"], item["far"] = {}, {}
-            for j in [*range(1, place.outer), 0]:
-                for k in range(1, place.inner):
-                    at = j * (place.inner - 1) + k - 1
-                    copy = remote(
-                        stage.at[place.slot(j, k)],
-                        near_box.at[at],
-                        si.at[at],
-                        ri.at[at],
-                        "tensor",
-                        place.slot(0, k),
-                    )
-                    copy.start()
-                    item["near"][j, k] = copy
+            for c in range(item["pieces"]):
+
+                @pl.loop(0, item["size"] // size)
+                def _(step, c=c, x=x, stage=stage, part=part, size=size, item=item):
+                    at = pl.ds(pl.multiple_of(c * item["size"] + step * size, size), size)
+                    for n in range(tensor_count):
+                        stage[n, at, :] = x[at, n * part : (n + 1) * part]
+
+                rows = pl.ds(c * item["size"], item["size"])
+                for j in [*range(1, place.outer), 0]:
+                    for k in range(1, place.inner):
+                        at = j * (place.inner - 1) + k - 1
+                        copy = remote(
+                            stage.at[place.slot(j, k), rows],
+                            near_box.at[at, rows],
+                            si.at[c * n_near + at],
+                            ri.at[c * n_near + at],
+                            "tensor",
+                            place.slot(0, k),
+                        )
+                        copy.start()
+                        item["near"][c, j, k] = copy
         for item in sums:
             place = places["tensor"]
             out = outs[item["out"]]
             stage, near_box, outgoing, far_box, si, ri, so, ro = work[
                 item["scratch"] : item["scratch"] + 8
             ]
-            rows = stage.shape[1]
-            size = row_chunk(rows)
-            for j in [*range(1, place.outer), 0]:
-                for k in range(1, place.inner):
-                    item["near"][j, k].wait_recv()
-
-                @pl.loop(0, rows // size)
-                def _(step, j=j):
-                    at = pl.ds(pl.multiple_of(step * size, size), size)
-                    value = stage[place.slot(j, 0), at, :].astype(jnp.float32)
+            size = row_chunk(item["size"])
+            for c in range(item["pieces"]):
+                rows = pl.ds(c * item["size"], item["size"])
+                for j in [*range(1, place.outer), 0]:
                     for k in range(1, place.inner):
-                        value += near_box[j * (place.inner - 1) + k - 1, at, :].astype(jnp.float32)
+                        item["near"][c, j, k].wait_recv()
+
+                    @pl.loop(0, item["size"] // size)
+                    def _(step, c=c, j=j, item=item, size=size):
+                        at = pl.ds(pl.multiple_of(c * item["size"] + step * size, size), size)
+                        value = stage[place.slot(j, 0), at, :].astype(jnp.float32)
+                        for k in range(1, place.inner):
+                            value += near_box[j * (place.inner - 1) + k - 1, at, :].astype(
+                                jnp.float32
+                            )
+                        if j:
+                            outgoing[j, at, :] = value.astype(outgoing.dtype)
+                        else:
+                            out[at, :] = value
+
                     if j:
-                        outgoing[j, at, :] = value.astype(outgoing.dtype)
-                    else:
-                        out[at, :] = value
-
-                if j:
-                    copy = remote(
-                        outgoing.at[j], far_box.at[j], so.at[j], ro.at[j], "tensor", place.slot(j, 0)
-                    )
-                    copy.start()
-                    item["far"][j] = copy
-        for entry in plan:
+                        copy = remote(
+                            outgoing.at[j, rows],
+                            far_box.at[j, rows],
+                            so.at[c * place.outer + j],
+                            ro.at[c * place.outer + j],
+                            "tensor",
+                            place.slot(j, 0),
+                        )
+                        copy.start()
+                        item["far"][c, j] = copy
+        for entry in sorted(plan, key=lambda entry: "held" not in entry):
             place = places[entry["axis"]]
             held = work[entry["held"]] if "held" in entry else outs[entry["out"]]
             so, ro, si, ri, own_sem = work[entry["sems"] : entry["sems"] + 5]
-            for j in range(1, place.outer):
-                entry["far"][j - 1].wait_recv()
-                block = held.at[place.slot(-j, 0)]
-                for k in range(1, place.inner):
-                    at = j * (place.inner - 1) + k - 1
-                    copy = remote(
-                        block, block, si.at[at], ri.at[at], place.axis, place.slot(0, k)
-                    )
-                    copy.start()
-                    entry["near"].append(copy)
+            for c in range(entry["pieces"]):
+                rows = pl.ds(c * entry["size"], entry["size"])
+                for j in range(1, place.outer):
+                    entry["far"][c * (place.outer - 1) + j - 1].wait_recv()
+                    block = held.at[place.slot(-j, 0), rows]
+                    for k in range(1, place.inner):
+                        at = (c * place.outer + j) * (place.inner - 1) + k - 1
+                        copy = remote(
+                            block, block, si.at[at], ri.at[at], place.axis, place.slot(0, k)
+                        )
+                        copy.start()
+                        entry["near"].append(copy)
+        for entry in plan:
             if "held" in entry:
-                finish(entry, ins, outs, held)
+                finish(entry, ins, outs, work[entry["held"]])
         for item in sums:
             out = outs[item["out"]]
             far_box = work[item["scratch"] + 3]
-            rows = out.shape[0]
-            size = row_chunk(rows)
-            for copy in item["far"].values():
-                copy.wait_recv()
-
-            @pl.loop(0, rows // size)
-            def _(step, out=out, far_box=far_box, size=size, item=item):
-                at = pl.ds(pl.multiple_of(step * size, size), size)
-                value = out[at, :]
-                for j in item["far"]:
-                    value += far_box[j, at, :].astype(jnp.float32)
-                out[at, :] = value
+            size = row_chunk(item["size"])
+            outer = places["tensor"].outer
+            for c in range(item["pieces"]):
+                for j in range(1, outer):
+                    item["far"][c, j].wait_recv()
+
+                @pl.loop(0, item["size"] // size)
+                def _(step, c=c, out=out, far_box=far_box, size=size, item=item):
+                    at = pl.ds(pl.multiple_of(c * item["size"] + step * size, size), size)
+                    value = out[at, :]
+                    for j in range(1, outer):
+                        value += far_box[j, at, :].astype(jnp.float32)
+                    out[at, :] = value
 
             for copy in [*item["near"].values(), *item["far"].values()]:
                 copy.wait_send()
@@ -540,14 +588,20 @@
         ],
         axis=1,
     )
-    hook_all, factor_all = communicate(
-        "adapter_sums",
+    input_terms = (
+        dot(query_rows_gradient, w_query_all, contract_cols)
+        + dot(key_rows_gradient, w_key_all, contract_cols)
+        + dot(value_rows_gradient, w_value_all, contract_cols)
+    ).astype(bf16)
+    hook_all, factor_all, grad_normed = communicate(
+        "scatter_grad",
         6,
         counts,
         gathers=[
             (hook_terms.astype(bf16), "tensor", "vmem"),
             (factor_terms.astype(bf16), "dp", "vmem"),
         ],
+        reduces=[input_terms],
     )
     factor_gradient = jnp.sum(factor_all.astype(f32), axis=0)
     query_factor_gradient = factor_gradient[:, : query_second_factor.shape[1]]
@@ -557,31 +611,22 @@
     slice_rows = full_width // (counts["dp"] * counts["tensor"])
     adapter_term = adapter_term.reshape(counts["dp"], counts["tensor"], slice_rows, -1)
     adapter_mine = lax.dynamic_index_in_dim(adapter_term, tensor_rank, 1, keepdims=False)
-    input_terms = (
-        dot(query_rows_gradient, w_query_all, contract_cols)
-        + dot(key_rows_gradient, w_key_all, contract_cols)
-        + dot(value_rows_gradient, w_value_all, contract_cols)
-    ).astype(bf16)
-    adapter_blocks, grad_normed = communicate(
-        "scatter_grad",
-        7,
-        counts,
-        gathers=[(adapter_mine.astype(bf16), "dp", "vmem")],
-        reduces=[input_terms],
-    )
-    adapter_rows = jnp.sum(
-        lax.dynamic_index_in_dim(adapter_blocks, data_rank, 1, keepdims=False).astype(f32), axis=0
-    )
     a_local = lax.dynamic_slice_in_dim(a_both, tensor_rank * part_width, part_width)
     grad_normed = grad_normed + dot(hook, a_local, contract_cols)
     narrow = pol_hidden.astype(f32)
     pre_sums = jnp.sum(narrow * pre_local * grad_normed, axis=1)
     pre_sums = jnp.pad(pre_sums[None, :], ((0, 7), (0, 0)))
-    adapter_all, pre_all = communicate(
-        "last_sums",
-        8,
+    adapter_blocks, pre_all = communicate(
+        "adapter_parts",
+        7,
         counts,
-        gathers=[(adapter_rows.astype(bf16), "tensor", "vmem"), (pre_sums, "tensor", "vmem")],
+        gathers=[(adapter_mine.astype(bf16), "dp", "vmem"), (pre_sums, "tensor", "vmem")],
+    )
+    adapter_rows = jnp.sum(
+        lax.dynamic_index_in_dim(adapter_blocks, data_rank, 1, keepdims=False).astype(f32), axis=0
+    )
+    (adapter_all,) = communicate(
+        "adapter_gather", 8, counts, gathers=[(adapter_rows.astype(bf16), "tensor", "vmem")]
     )
     grad_a = adapter_all.reshape(-1, adapter_all.shape[-1]).astype(f32)
     pre_dot = jnp.sum(pre_all[:, 0, :], axis=0)

time: 457 us -> 410 us (0.90)
  Pallas kernels: 353 us -> 305 us
    pallas_call x8, Pallas kernels: 353 us -> 305 us  [communicate(): pl.pallas_call(kernel, name=name, out_shape=out_shapes, in_specs=in_specs...]
where the time goes in v2:
time: 410 us; the launch traced here: 409 us
  Pallas kernels  305 us (74%)
  matrix products  51.2 us (12%)
  local copies, waits for them, and re-layouts  28.7 us (7%)
  other arithmetic  23.2 us (6%)
    pallas_call x8, Pallas kernels, communicate(): pl.pallas_call(kernel, name=name, out_shape=out_shapes, in_specs=in_specs...  305 us
    dot_general x17, matrix products, dot(): return lax.dot_general(a, b, dims, preferred_element_type=f32)  44.1 us

profile of v2, /device:TPU:0, one launch (start us, length us, event | category | flops | bytes accessed | tf_op | source)
XLA Modules:
  0.0 409.3 jit_solution(5733994762332524770)
XLA Ops:
  0.7 0.8 pad_add_fusion
  2.1 0.7 fusion.99
  2.9 0.8 dynamic_slice.20
  3.6 0.8 dynamic_slice.22
  4.4 1.3 reshape.314.refs_3_
  6.1 1.1 copy.83
  7.3 1.1 copy.84
  8.4 0.9 pad_maximum_fusion.1.refs_0_
  9.4 1.2 mul.555
  11.6 99.1 %gather_inputs.1 = (bf16[4,1152,128]{2,1,0:T(8,128)(2,1)}, bf16[4,1152,512]{2,1,0:T(8,128)(2,1)}, bf16[576,4608]{1,0:T(8,128)(2,1)}, f32[576,1]{1,0:T(8,128)}, b...) custom-call(bf16[1152,128]{1,0:T(8,128)(2,1)} %pad_maximum_fusion.1.refs_0_, ...), custom_call_target="tpu_custom_call" | custom-call | tf_op jit(solution)/shard_map/gather_inputs/pallas_call | solution.py:426
  110.7 1.1 slice_reduce_fusion
  111.8 3.1 fusion.20
  115.1 4.0 fusion.17
  119.6 6.3 %convolution_add_fusion.2 = f32[576,512]{1,0:T(8,128)S(1)} fusion(bf16[576,4608]{1,0:T(8,128)(2,1)} %get-tuple-element.19, bf16[4608,512]{1,0:T(8,128)(2,1)} %bitcast.129, f32[288,512]{1,0:T(8,128)S(1)} %convolution_multiply_fusion.1), kind=kOutput, calls=%fused_computation.20 | convolution fusion | flops 2718203904 | bytes 11796480 | tf_op jit(solution)/shard_map/dot_general | solution.py:470
  126.2 0.8 subtract_convert_fusion
  127.5 0.9 copy.86
  128.4 0.9 copy.87
  129.3 0.8 copy.100
  130.1 2.5 copy.85
  132.6 4.3 %fusion.116 = f32[6,96,2,128]{3,1,2,0:T(8,128)S(1)} fusion(bf16[6,96,4608,1]{2,1,3,0:T(8,128)(2,1)} %bitcast.139, bf16[2,128,4608,1]{2,1,0,3:T(8,128)(2,1)} %bitcast.134), kind=kOutput, calls=%fused_computation.185 | convolution fusion | flops 1358954496 | bytes 8257536 | tf_op jit(solution)/shard_map/dot_general | solution.py:470
  137.2 0.7 copy-done.16
  138.3 0.9 fusion.24
  139.2 1.4 fusion.113
  141.4 1.0 reshape_reshape.6
  142.4 1.9 slice_bitcast_fusion
  144.3 3.0 copy.102
  147.3 7.8 %convolution_convert_fusion.refs_0_ = bf16[576,4608]{1,0:T(8,128)(2,1)} fusion(bf16[576,512]{1,0:T(8,128)(2,1)} %reshape_reshape.6, bf16[4608,512]{1,0:T(8,128)(2,1)} %bitcast.148), kind=kOutput, calls=%fused_computation.1 | convolution fusion | flops 2720563200 | bytes 10616832 | tf_op jit(solution)/shard_map/dot_general | solution.py:470
  155.1 74.4 %scatter_out.1 = f32[576,576]{1,0:T(8,128)} custom-call(bf16[576,4608]{1,0:T(8,128)(2,1)} %convolution_convert_fusion.refs_0_), custom_call_target="tpu_custom_call" | custom-call | tf_op jit(solution)/shard_map/scatter_out/pallas_call | solution.py:426
  229.5 2.3 multiply_reduce_fusion.1
  231.9 0.7 maximum_maximum_fusion.refs_0_
  232.6 10.0 %token_sums.1 = f32[8,8,288]{2,1,0:T(8,128)} custom-call(f32[8,288]{1,0:T(8,128)} %maximum_maximum_fusion.refs_0_), custom_call_target="tpu_custom_call" | custom-call | tf_op jit(solution)/shard_map/token_sums/pallas_call | solution.py:426
  242.6 0.9 reduce_sum.151
  243.9 0.9 slice_bitcast_fusion.1
  245.6 5.8 %sequence_scores.1 = f32[4,8,128]{2,1,0:T(8,128)} custom-call(f32[8,128]{1,0:T(8,128)} %pad.18.refs_0_), custom_call_target="tpu_custom_call" | custom-call | tf_op jit(solution)/shard_map/sequence_scores/pallas_call | solution.py:426
  251.4 0.7 slice_bitcast_fusion.3
  252.7 0.6 fusion.101
  253.8 1.0 subtract_convert_fusion.1.refs_0_
  254.8 46.4 %gather_grad.1 = bf16[288,4608]{1,0:T(8,128)(2,1)} custom-call(bf16[288,576]{1,0:T(8,128)(2,1)} %subtract_convert_fusion.1.refs_0_), custom_call_target="tpu_custom_call" | custom-call | tf_op jit(solution)/shard_map/gather_grad/pallas_call | solution.py:426
  301.3 5.4 %convolution_convert_fusion.2 = bf16[288,512]{1,0:T(8,128)(2,1)} fusion(bf16[288,4608]{1,0:T(8,128)(2,1)} %gather_grad.1, bf16[4608,512]{1,0:T(8,128)(2,1)} %bitcast.149), kind=kOutput, calls=%fused_computation.31 | convolution fusion | flops 1359101952 | bytes 7667712 | tf_op jit(solution)/shard_map/dot_general | solution.py:470
  306.7 1.1 reshape_reshape.7
  308.5 1.2 convolution_bitcast_fusion
  309.7 2.3 fusion.25
  312.0 2.2 convolution_bitcast_fusion.1
  315.0 0.8 multiply_subtract_fusion
  316.5 0.7 fusion.68.refs_1_
  317.4 0.7 fusion.81.refs_0_
  318.1 4.1 fusion.47
  322.2 0.9 convolution_add_fusion.1
  323.1 0.8 copy-done.10
  323.9 2.4 fusion.1.refs_2_
  326.3 47.6 %scatter_grad.1 = (bf16[8,288,128]{2,1,0:T(8,128)(2,1)}, bf16[4,64,768]{2,1,0:T(8,128)(2,1)}, f32[288,576]{1,0:T(8,128)}) custom-call(bf16[288,128]{1,0:T(8,128)(2,1)} %fusion.81.refs_0_, bf16[64,768]{1,0:T(8,128)(2,1)} %fusion.68.refs_1_, bf16[288,4608]{1,0:T(8,128)(2,1)} %fusion.1.refs_2_), custom_call_target="tpu_custom_call" | custom-call | tf_op jit(solution)/shard_map/scatter_grad/pallas_call | solution.py:426
  373.9 1.1 reduce_sum.157
  375.0 3.2 fusion.2
  378.2 1.4 fusion.35
  379.6 0.7 fusion.73.refs_0_
  380.3 0.6 pad.19.refs_1_
  380.9 0.6 slice.173
  381.6 0.7 slice.172
  382.2 10.2 %adapter_parts.1 = (bf16[4,4,144,128]{3,2,1,0:T(8,128)(2,1)}, f32[8,8,288]{2,1,0:T(8,128)}) custom-call(bf16[4,144,128]{2,1,0:T(8,128)(2,1)} %fusion.73.refs_0_, f32[8,288]{1,0:T(8,128)} %pad.19.refs_1_), custom_call_target="tpu_custom_call" | custom-call | tf_op jit(solution)/shard_map/adapter_parts/pallas_call | solution.py:426
  392.4 0.9 slice_reduce_fusion.1
  393.3 1.1 fusion.33
  394.4 1.6 dynamic-slice_reduce_fusion.refs_0_
  396.0 11.5 %adapter_gather.1 = bf16[8,144,128]{2,1,0:T(8,128)(2,1)} custom-call(bf16[144,128]{1,0:T(8,128)(2,1)} %dynamic-slice_reduce_fusion.refs_0_), custom_call_target="tpu_custom_call" | custom-call | tf_op jit(solution)/shard_map/adapter_gather/pallas_call | solution.py:426
  407.5 1.8 bitcast_convert_fusion
  (109 shorter events, 9.6 us)
Async XLA Ops:
  0.6 118.7 %copy-start = (bf16[64,512]{1,0:T(8,128)(2,1)S(1)}, bf16[64,512]{1,0:T(8,128)(2,1)}, u32[]{:S(2)}) copy-start(bf16[64,512]{1,0:T(8,128)(2,1)} %param.28) | copy-start | bytes 196612
  0.6 8.6 %copy-start.6 = (bf16[288,576]{1,0:T(8,128)(2,1)S(1)}, bf16[288,576]{1,0:T(8,128)(2,1)}, u32[]{:S(2)}) copy-start(bf16[288,576]{1,0:T(8,128)(2,1)} %param.17) | copy-start | bytes 995332
  9.3 1.3 copy-start.19
  9.3 1.3 copy-start.8
  10.7 0.9 copy-start.4
  111.8 3.1 copy-start.22
  111.8 3.3 copy-start.9
  127.5 2.6 copy-start.2
  136.9 1.1 copy-start.16
  136.9 1.3 copy-start.17
  137.2 1.9 copy-start.20
  137.2 1.9 copy-start.21
  139.1 1.4 copy-start.13
  140.5 0.8 copy-start.11
  229.5 2.5 copy-start.25
  229.5 14.0 %copy-start.1 = (f32[576,576]{1,0:T(8,128)S(1)}, f32[576,576]{1,0:T(8,128)}, u32[]{:S(2)}) copy-start(f32[576,576]{1,0:T(8,128)} %scatter_out.1) | copy-start | bytes 3981316
  229.5 14.0 %copy-start.5 = (bf16[576,576]{1,0:T(8,128)(2,1)S(1)}, bf16[576,576]{1,0:T(8,128)(2,1)}, u32[]{:S(2)}) copy-start(bf16[576,576]{1,0:T(8,128)(2,1)} %copy-done.4) | copy-start | bytes 1990660
  243.9 8.4 %copy-start.26 = (s32[12]{0:T(128)S(1)}, s32[12]{0:T(128)}, u32[]{:S(2)}) copy-start(s32[12]{0:T(128)} %param.19) | copy-start | bytes 148
  243.9 9.8 %copy-start.24 = (s32[3]{0:T(128)S(1)}, s32[3]{0:T(128)}, u32[]{:S(2)}) copy-start(s32[3]{0:T(128)} %param.18) | copy-start | bytes 40
  243.9 9.9 %copy-start.7 = (bf16[288,576]{1,0:T(8,128)(2,1)S(1)}, bf16[288,576]{1,0:T(8,128)(2,1)}, u32[]{:S(2)}) copy-start(bf16[288,576]{1,0:T(8,128)(2,1)} %param.17) | copy-start | bytes 995332
  301.2 6.6 %copy-start.12 = (bf16[6,2,2,96,96]{3,4,2,1,0:T(8,128)(2,1)S(1)}, bf16[6,2,2,96,96]{3,4,2,1,0:T(8,128)(2,1)}, u32[]{:S(2)}) copy-start(bf16[6,2,2,96,96]{3,4,2,1,0:T(8,128)(2,1)} %copy-done.11) | copy-start | bytes 1327108
  306.7 3.0 copy-start.14
  312.0 2.7 copy-start.23
  318.1 4.1 copy-start.3
  322.2 1.7 copy-start.10
  375.0 3.2 copy-start.15
  378.2 2.7 copy-start.18
